TPU v7x, 32 devices: a whole 2x2x4 slice. The times are simulated.
32 devices in a mesh: gx: 4 (over z), gy: 8 (over y, x, core).
Axes of the slice: x: 2, y: 2, z: 4, core: 2. Of those that a mesh axis runs over, the one named last changes fastest.
Arguments:
- velocity: float32 [3, 32, 64, 1024], P(None, None, 'gx', 'gy'), may hold values from -6 to 6
- old_tendency: float32 [3, 32, 64, 1024], P(None, None, 'gx', 'gy'), may hold values from -6 to 6
- obstacle: int32 [32, 64, 1024], P(None, 'gx', 'gy'), may hold values 0 or 1
Outputs:
- corrected: float32 [3, 32, 64, 1024], P(None, None, 'gx', 'gy')
- pressure: float32 [32, 64, 1024], P(None, 'gx', 'gy')
Inputs may be any that keep to these rules, and one draw needn't show every extreme that they name: `obstacle`: 1 marks a building cell, 0 a fluid cell.
All inputs are finite; a program needn't handle non-finite values. No bound on the sum of `obstacle` on one device may be relied on, other than what follows from the above.
Results may differ from a plain program's by a relative error of at most 0.00002.
Values sent between devices are 32-bit elements; how exact they have to be, the bound alone decides.
A program may use at most 128 MiB of HBM per device.

v0:
```python
import functools

import jax
import jax.numpy as jnp
from jax import lax
from jax.experimental import pallas as pl
from jax.experimental.pallas import tpu as pltpu
from jax.sharding import PartitionSpec as P

LEVELS = 3
SWEEPS = 2
COARSE_SWEEPS = 8
VISCOSITY = 0.1
TIME_STEP = 0.25
WEIGHT_NEW = 15.0 / 16.0
WEIGHT_OLD = -25.0 / 48.0
HELMHOLTZ = 0.0001

LANES = 128
SUB = 8
HALO_X = 8
HALO_Y = 24
MESH = pl.DeviceIdType.MESH


def iota2(shape, dim):
    return lax.broadcasted_iota(jnp.int32, shape, dim)


def restrict_matrix(rows, cols, nz, period):
    i, o = iota2((rows, cols), 0), iota2((rows, cols), 1)
    o = o % period
    half = nz // 2
    hit = ((i // nz) // 2 == o // half) & ((i % nz) // 2 == o % half)
    return jnp.where(hit, 0.125, 0.0).astype(jnp.float32)


def prolong_matrix(rows, cols, nz):
    i, o = iota2((rows, cols), 0), iota2((rows, cols), 1)
    half = nz // 2
    hit = ((o // nz) // 2 == i // half) & ((o % nz) // 2 == i % half)
    return jnp.where(hit, 1.0, 0.0).astype(jnp.float32)


def mm(a, b):
    return jnp.dot(a, b, precision=lax.Precision.HIGHEST, preferred_element_type=jnp.float32)


class Level:
    def __init__(self, level, nz):
        self.nz = nz
        self.scale = 1.0 / float(4**level)
        lane = iota2((SUB, LANES), 1)
        row = iota2((SUB, LANES), 0)
        self.lane = lane
        self.row = row
        z = lane % nz
        self.not_top = z < nz - 1
        self.not_bottom = z > 0
        parity = (z + lane // nz + row) % 2
        self.colour = [parity == 0, parity == 1]
        edge = (z == 0) | (z == nz - 1)
        diag_in = HELMHOLTZ + 6.0 * self.scale
        diag_edge = HELMHOLTZ + 5.0 * self.scale
        self.diag = jnp.where(edge, diag_edge, diag_in).astype(jnp.float32)
        self.inv = jnp.where(edge, 1.0 / diag_edge, 1.0 / diag_in).astype(jnp.float32)
        self.take = jnp.where(
            edge, self.scale / diag_edge, self.scale / diag_in
        ).astype(jnp.float32)

    def x_plus(self, tiles, t):
        n = len(tiles)
        both = tiles[t] if n == 1 else jnp.where(self.lane < self.nz, tiles[(t + 1) % n], tiles[t])
        return pltpu.roll(both, LANES - self.nz, 1)

    def x_minus(self, tiles, t):
        n = len(tiles)
        last = self.lane >= LANES - self.nz
        both = tiles[t] if n == 1 else jnp.where(last, tiles[(t - 1) % n], tiles[t])
        return pltpu.roll(both, self.nz, 1)

    def y_plus(self, tile, following):
        return pltpu.roll(jnp.where(self.row == 0, following, tile), SUB - 1, 0)

    def y_minus(self, tile, previous):
        return pltpu.roll(jnp.where(self.row == SUB - 1, previous, tile), 1, 0)

    def z_plus(self, tile):
        return jnp.where(self.not_top, pltpu.roll(tile, LANES - 1, 1), 0.0)

    def z_minus(self, tile):
        return jnp.where(self.not_bottom, pltpu.roll(tile, 1, 1), 0.0)


def tile_of(t):
    return slice(t * LANES, (t + 1) * LANES)


def row_loop(tiles, unroll, body):
    while tiles % unroll:
        unroll -= 1

    def step(i, carry):
        for k in range(unroll):
            body(pl.multiple_of((i * unroll + k) * SUB, SUB))
        return carry

    lax.fori_loop(0, tiles // unroll, step, 0)


def neighbours(lv, p, r, tiles, t):
    cols = tile_of(t)
    here = tiles[t]
    up = lv.y_plus(here, p[pl.ds(r + 2 * SUB, SUB), cols])
    down = lv.y_minus(here, p[pl.ds(r, SUB), cols])
    return (
        lv.x_plus(tiles, t)
        + lv.x_minus(tiles, t)
        + up
        + down
        + lv.z_plus(here)
        + lv.z_minus(here)
    )


def wrap_rows(p):
    rows = p.shape[0]
    p[0:SUB, :] = p[rows - 2 * SUB : rows - SUB, :]
    p[rows - SUB : rows, :] = p[SUB : 2 * SUB, :]


def first_half(lv, p, f, unroll):
    def body(r):
        for t in range(p.shape[1] // LANES):
            p[pl.ds(r + SUB, SUB), tile_of(t)] = jnp.where(
                lv.colour[0], f[pl.ds(r, SUB), tile_of(t)] * lv.inv, 0.0
            )

    row_loop(f.shape[0] // SUB, unroll, body)


def half_sweep(lv, p, f, colour, unroll, wrap, trim_rows=0, trim_tiles=0):
    if wrap:
        wrap_rows(p)
    count = p.shape[1] // LANES

    def body(start):
        r = start + trim_rows
        tiles = [p[pl.ds(r + SUB, SUB), tile_of(t)] for t in range(count)]
        for t in range(trim_tiles, count - trim_tiles):
            total = neighbours(lv, p, r, tiles, t)
            new = f[pl.ds(r, SUB), tile_of(t)] * lv.inv + total * lv.take
            p[pl.ds(r + SUB, SUB), tile_of(t)] = (
                jnp.where(lv.colour[0], tiles[t], new) if colour else jnp.where(lv.colour[0], new, tiles[t])
            )

    row_loop((f.shape[0] - 2 * trim_rows) // SUB, unroll, body)


def presmooth(lv, p, f, sweeps, unroll, wrap):
    first_half(lv, p, f, unroll)
    for k in range(1, 2 * sweeps):
        half_sweep(lv, p, f, k % 2, unroll, wrap)


def postsmooth(lv, p, f, unroll, wrap, trim_rows=0, trim_tiles=0):
    for k in range(2 * SWEEPS):
        half_sweep(lv, p, f, k % 2, unroll, wrap, trim_rows, trim_tiles)


def residual(lv, p, f, out, first, last, unroll, wrap):
    if wrap:
        wrap_rows(p)
    count = p.shape[1] // LANES

    def body(r):
        tiles = [p[pl.ds(r + SUB, SUB), tile_of(t)] for t in range(count)]
        for t in range(first, last):
            total = neighbours(lv, p, r, tiles, t)
            out[pl.ds(r, SUB), tile_of(t - first)] = f[pl.ds(r, SUB), tile_of(t)] - (
                lv.diag * tiles[t] - lv.scale * total
            )

    row_loop(f.shape[0] // SUB, unroll, body)


def restrict_rows(value, pairs, start, count, emit):
    for t in range(value.shape[1] // LANES):
        pairs[t, 0 : value.shape[0], :] = value[:, tile_of(t)]
        emit(
            t,
            pairs[t, pl.ds(start, count, stride=2), :]
            + pairs[t, pl.ds(start + 1, count, stride=2), :],
        )


def prolong_rows(value, pairs, p, first):
    rows = value.shape[0]
    for k in range(value.shape[1] // LANES):
        t = first + k
        pairs[t, pl.ds(0, rows, stride=2), :] = value[:, tile_of(k)]
        pairs[t, pl.ds(1, rows, stride=2), :] = value[:, tile_of(k)]
        p[SUB : SUB + 2 * rows, tile_of(t)] += pairs[t, 0 : 2 * rows, :]


def kernel(
    nx_dev, ny_dev, nz, nx, ny,
    vel_in, old_in, obs_in, cor_out, pre_out,
    vel, old, fluid, edge, edge_in, pred,
    f0, p0, r0, f1, p1, r1, f2, p2, r2, f3, p3, pairs,
    send_sem, recv_sem,
):
    gx, gy = lax.axis_index("gx"), lax.axis_index("gy")

    def device(dx, dy):
        return (lax.rem(gx + dx + nx_dev, nx_dev), lax.rem(gy + dy + ny_dev, ny_dev))

    peers = [(d, 0) for d in range(1, nx_dev)] + [(0, d) for d in range(1, ny_dev)]
    peers += [(a, b) for a in (-1, 1) for b in (-1, 1)]
    barrier = pltpu.get_barrier_semaphore()
    for dx, dy in peers:
        pl.semaphore_signal(barrier, inc=1, device_id=device(dx, dy), device_id_type=MESH)

    number = [0]

    def send(src, dst, dx, dy):
        k = number[0]
        number[0] += 1
        copy = pltpu.make_async_remote_copy(
            src_ref=src, dst_ref=dst, send_sem=send_sem.at[k], recv_sem=recv_sem.at[k],
            device_id=device(dx, dy), device_id_type=MESH,
        )
        copy.start()
        return copy

    per = LANES // nz
    blocks = nx // per
    width = blocks * LANES
    lv0 = Level(0, nz)
    lane = lv0.lane

    def load_tile(ref, base, t):
        rows = [ref[pl.ds(base + t * per + i, nz, stride=nx), :] for i in range(per)]
        return jnp.concatenate(rows, axis=0).T

    for c in range(3):
        for t in range(blocks):
            vel[c, SUB : SUB + ny, tile_of(t + 1)] = load_tile(vel_in, c * nz * nx, t)

    pltpu_wait = functools.partial(pl.semaphore_wait, barrier)
    pltpu_wait(len(peers))

    def join(high):
        parts = []
        for c in range(3):
            source = vel[c, SUB : SUB + ny, tile_of(blocks if high else 1)]
            start = LANES - nz if high else 0
            parts.append(pltpu.roll(source, (c * nz - start) % LANES, 1))
        wide = iota2((ny, LANES), 1)
        return jnp.where(wide < nz, parts[0], jnp.where(wide < 2 * nz, parts[1], parts[2]))

    copies = [
        send(vel.at[:, ny : ny + SUB, LANES : LANES + width], vel.at[:, 0:SUB, LANES : LANES + width], 0, 1),
        send(
            vel.at[:, SUB : 2 * SUB, LANES : LANES + width],
            vel.at[:, SUB + ny : 2 * SUB + ny, LANES : LANES + width], 0, -1,
        ),
    ]
    edge[0] = join(True)
    copies.append(send(edge.at[0], edge_in.at[0], 1, 0))
    edge[1] = join(False)
    copies.append(send(edge.at[1], edge_in.at[1], -1, 0))

    for c in range(3):
        for t in range(blocks):
            old[c, :, tile_of(t)] = load_tile(old_in, c * nz * nx, t)
    for t in range(blocks):
        fluid[:, tile_of(t)] = (1 - load_tile(obs_in, 0, t)).astype(jnp.float32)
    for copy in copies:
        copy.wait()
    for c in range(3):
        vel[c, SUB : SUB + ny, tile_of(0)] = pltpu.roll(edge_in[0], (LANES - nz - c * nz) % LANES, 1)
        vel[c, SUB : SUB + ny, tile_of(blocks + 1)] = pltpu.roll(edge_in[1], (-c * nz) % LANES, 1)

    def momentum(r):
        here = [
            [vel[c, pl.ds(r + SUB, SUB), tile_of(t)] for t in range(blocks + 2)] for c in range(3)
        ]
        for t in range(1, blocks + 1):
            cols = tile_of(t)
            wet = fluid[pl.ds(r, SUB), tile_of(t - 1)]
            for c in range(3):
                q = here[c][t]
                xp, xm = lv0.x_plus(here[c], t), lv0.x_minus(here[c], t)
                yp = lv0.y_plus(q, vel[c, pl.ds(r + 2 * SUB, SUB), cols])
                ym = lv0.y_minus(q, vel[c, pl.ds(r, SUB), cols])
                zp, zm = lv0.z_plus(q), lv0.z_minus(q)
                advect = 0.5 * (
                    here[0][t] * (xp - xm) + here[1][t] * (yp - ym) + here[2][t] * (zp - zm)
                )
                diffuse = xp + xm + yp + ym + zp + zm - 6.0 * q
                tendency = VISCOSITY * diffuse - advect
                pred[c, pl.ds(r + SUB, SUB), cols] = wet * (
                    q
                    + TIME_STEP
                    * (WEIGHT_NEW * tendency + WEIGHT_OLD * old[c, pl.ds(r, SUB), tile_of(t - 1)])
                )

    row_loop(ny // SUB, 2, momentum)

    inner = slice(LANES, LANES + width)
    copies = [
        send(pred.at[0, SUB : SUB + ny, tile_of(blocks)], pred.at[0, SUB : SUB + ny, tile_of(0)], 1, 0),
        send(pred.at[0, SUB : SUB + ny, tile_of(1)], pred.at[0, SUB : SUB + ny, tile_of(blocks + 1)], -1, 0),
        send(pred.at[1, ny : ny + SUB, inner], pred.at[1, 0:SUB, inner], 0, 1),
        send(pred.at[1, SUB : 2 * SUB, inner], pred.at[1, SUB + ny : 2 * SUB + ny, inner], 0, -1),
    ]
    for copy in copies:
        copy.wait()

    side = HALO_X // per
    hx = side * LANES

    def divergence(r):
        u = [pred[0, pl.ds(r + SUB, SUB), tile_of(t)] for t in range(blocks + 2)]
        for t in range(1, blocks + 1):
            cols = tile_of(t)
            v = pred[1, pl.ds(r + SUB, SUB), cols]
            w = pred[2, pl.ds(r + SUB, SUB), cols]
            v_plus = lv0.y_plus(v, pred[1, pl.ds(r + 2 * SUB, SUB), cols])
            v_minus = lv0.y_minus(v, pred[1, pl.ds(r, SUB), cols])
            total = (
                (lv0.x_plus(u, t) - lv0.x_minus(u, t))
                + (v_plus - v_minus)
                + (lv0.z_plus(w) - lv0.z_minus(w))
            )
            f0[pl.ds(r + HALO_Y, SUB), tile_of(t - 1 + side)] = total * (-0.5 / TIME_STEP)

    row_loop(ny // SUB, 2, divergence)

    span = {
        0: (slice(HALO_Y, HALO_Y + ny), slice(HALO_Y, HALO_Y + ny)),
        1: (slice(ny, ny + HALO_Y), slice(0, HALO_Y)),
        -1: (slice(HALO_Y, 2 * HALO_Y), slice(HALO_Y + ny, 2 * HALO_Y + ny)),
    }
    cross = {
        0: (slice(hx, hx + width), slice(hx, hx + width)),
        1: (slice(width, width + hx), slice(0, hx)),
        -1: (slice(hx, 2 * hx), slice(hx + width, 2 * hx + width)),
    }
    copies = []
    for dx, dy in ((1, 0), (-1, 0), (0, 1), (0, -1), (1, 1), (1, -1), (-1, 1), (-1, -1)):
        copies.append(
            send(f0.at[span[dy][0], cross[dx][0]], f0.at[span[dy][1], cross[dx][1]], dx, dy)
        )
    lv1, lv2, lv3 = Level(1, nz // 2), Level(2, nz // 4), Level(3, nz // 8)
    zero_rows = jnp.zeros((SUB, p0.shape[1]), jnp.float32)
    p0[0:SUB, :] = zero_rows
    p0[p0.shape[0] - SUB :, :] = zero_rows
    p1[0:SUB, :] = zero_rows[:, : p1.shape[1]]
    p1[p1.shape[0] - SUB :, :] = zero_rows[:, : p1.shape[1]]
    for copy in copies:
        copy.wait()

    presmooth(lv0, p0, f0, SWEEPS, 2, False)
    residual(lv0, p0, f0, r0, side, side + blocks, 2, False)
    rows1 = f1.shape[0]
    down1 = mm(r0[...], restrict_matrix(width, LANES, nz, LANES))

    def emit1(t, value):
        f1[:, tile_of(t)] = value

    restrict_rows(down1, pairs, 0, rows1, emit1)

    copies = [
        send(f1.at[:, tile_of(0)], f1.at[:, tile_of(j)], nx_dev - j, 0) for j in range(1, nx_dev)
    ]
    for copy in copies:
        copy.wait()
    presmooth(lv1, p1, f1, SWEEPS, 11, False)
    residual(lv1, p1, f1, r1, 0, nx_dev, 1, False)
    cols2 = f2.shape[1]
    down2 = mm(r1[...], restrict_matrix(r1.shape[1], cols2, nz // 2, cols2))
    own2 = ny // 4

    def emit2(t, value):
        f2[0:own2, tile_of(t)] = value

    restrict_rows(down2, pairs, HALO_Y // 2, own2, emit2)
    copies = [
        send(f2.at[0:own2, :], f2.at[j * own2 : (j + 1) * own2, :], 0, ny_dev - j)
        for j in range(1, ny_dev)
    ]
    for copy in copies:
        copy.wait()

    presmooth(lv2, p2, f2, SWEEPS, 16, True)
    residual(lv2, p2, f2, r2, 0, cols2 // LANES, 16, True)
    down3 = mm(r2[...], restrict_matrix(cols2, f3.shape[1], nz // 4, cols2 // 4))

    def emit3(t, value):
        f3[:, tile_of(t)] = value

    restrict_rows(down3, pairs, 0, f3.shape[0], emit3)
    presmooth(lv3, p3, f3, COARSE_SWEEPS, 16, True)
    rows3 = f3.shape[0]
    prolong_rows(
        mm(p3[SUB : SUB + rows3, :], prolong_matrix(p3.shape[1], cols2, nz // 4)), pairs, p2, 0
    )
    postsmooth(lv2, p2, f2, 16, True)
    wrap_rows(p2)

    first2 = SUB - HALO_Y // 4
    window = p2[first2 : first2 + rows1 // 2, :]
    prolong_rows(mm(window, prolong_matrix(cols2, r1.shape[1], nz // 2)), pairs, p1, 0)
    postsmooth(lv1, p1, f1, 11, False)

    lift = prolong_matrix(LANES, width, nz)
    body_rows = slice(SUB, SUB + rows1)
    prolong_rows(mm(p1[body_rows, tile_of(nx_dev - 1)], lift[:, width - hx :]), pairs, p0, 0)
    prolong_rows(mm(p1[body_rows, tile_of(0)], lift), pairs, p0, side)
    prolong_rows(mm(p1[body_rows, tile_of(1)], lift[:, :hx]), pairs, p0, side + blocks)
    postsmooth(lv0, p0, f0, 3, False, HALO_Y - SUB, side - 1)

    low = SUB + HALO_Y

    def correct(r):
        here = [
            p0[pl.ds(r + low, SUB), tile_of(t)] for t in range(side - 1, side + blocks + 1)
        ]
        for t in range(1, blocks + 1):
            cols = tile_of(t + side - 1)
            slope = (
                lv0.x_plus(here, t) - lv0.x_minus(here, t),
                lv0.y_plus(here[t], p0[pl.ds(r + low + SUB, SUB), cols])
                - lv0.y_minus(here[t], p0[pl.ds(r + low - SUB, SUB), cols]),
                lv0.z_plus(here[t]) - lv0.z_minus(here[t]),
            )
            wet = fluid[pl.ds(r, SUB), tile_of(t - 1)]
            for c in range(3):
                old[c, pl.ds(r, SUB), tile_of(t - 1)] = wet * (
                    pred[c, pl.ds(r + SUB, SUB), tile_of(t)] - (0.5 * TIME_STEP) * slope[c]
                )

    row_loop(ny // SUB, 2, correct)

    def store_tile(ref, base, t, value):
        turned = value.T
        for i in range(per):
            ref[pl.ds(base + t * per + i, nz, stride=nx), :] = turned[i * nz : (i + 1) * nz, :]

    for t in range(blocks):
        store_tile(pre_out, 0, t, p0[low : low + ny, tile_of(t + side)])
    for c in range(3):
        for t in range(blocks):
            store_tile(cor_out, c * nz * nx, t, old[c, :, tile_of(t)])


def body(nx_dev, ny_dev, velocity, old_tendency, obstacle):
    _, nz, nx, ny = velocity.shape
    rows0 = ny + 2 * HALO_Y
    wide0 = (nx + 2 * HALO_X) * nz
    width = nx * nz
    rows1, wide1 = rows0 // 2, nx_dev * (nx // 2) * (nz // 2)
    rows2, wide2 = ny_dev * ny // 4, nx_dev * (nx // 4) * (nz // 4)
    rows3 = rows2 // 2
    wide3 = max(LANES, wide2 // 4)
    tall = max(rows0, rows1, rows2)
    count = max(wide0, wide1, wide2, wide3) // LANES
    copies = 4 + 4 + 8 + (nx_dev - 1) + (ny_dev - 1)
    f32 = jnp.float32
    out = pl.pallas_call(
        functools.partial(kernel, nx_dev, ny_dev, nz, nx, ny),
        out_shape=(
            jax.ShapeDtypeStruct((3 * nz * nx, ny), f32),
            jax.ShapeDtypeStruct((nz * nx, ny), f32),
        ),
        in_specs=[pl.BlockSpec(memory_space=pltpu.VMEM)] * 3,
        out_specs=[pl.BlockSpec(memory_space=pltpu.VMEM)] * 2,
        scratch_shapes=[
            pltpu.VMEM((3, ny + 2 * SUB, width + 2 * LANES), f32),
            pltpu.VMEM((3, ny, width), f32),
            pltpu.VMEM((ny, width), f32),
            pltpu.VMEM((2, ny, LANES), f32),
            pltpu.VMEM((2, ny, LANES), f32),
            pltpu.VMEM((3, ny + 2 * SUB, width + 2 * LANES), f32),
            pltpu.VMEM((rows0, wide0), f32),
            pltpu.VMEM((rows0 + 2 * SUB, wide0), f32),
            pltpu.VMEM((rows0, width), f32),
            pltpu.VMEM((rows1, wide1), f32),
            pltpu.VMEM((rows1 + 2 * SUB, wide1), f32),
            pltpu.VMEM((rows1, wide1), f32),
            pltpu.VMEM((rows2, wide2), f32),
            pltpu.VMEM((rows2 + 2 * SUB, wide2), f32),
            pltpu.VMEM((rows2, wide2), f32),
            pltpu.VMEM((rows3, wide3), f32),
            pltpu.VMEM((rows3 + 2 * SUB, wide3), f32),
            pltpu.VMEM((count, tall, LANES), f32),
            pltpu.SemaphoreType.DMA((copies,)),
            pltpu.SemaphoreType.DMA((copies,)),
        ],
        compiler_params=pltpu.CompilerParams(
            collective_id=0, has_side_effects=True, vmem_limit_bytes=60 * 1024 * 1024
        ),
    )(
        velocity.reshape(3 * nz * nx, ny),
        old_tendency.reshape(3 * nz * nx, ny),
        obstacle.reshape(nz * nx, ny),
    )
    return out[0].reshape(3, nz, nx, ny), out[1].reshape(nz, nx, ny)


def solution(mesh):
    placed = (P(None, None, "gx", "gy"), P(None, None, "gx", "gy"), P(None, "gx", "gy"))
    return jax.shard_map(
        functools.partial(body, mesh.shape["gx"], mesh.shape["gy"]),
        mesh=mesh,
        in_specs=placed,
        out_specs=(P(None, None, "gx", "gy"), P(None, "gx", "gy")),
        check_vma=False,
    )
```

profile of v0, /device:TPU:0, one launch (start us, length us, event | category | flops | bytes accessed | tf_op | source)
XLA Modules:
  0.0 75.1 jit_solution(16527690337368176835)
XLA Ops:
  0.6 71.6 %shard_map.50 = (f32[1536,128]{1,0:T(8,128)}, f32[512,128]{1,0:T(8,128)}) custom-call(f32[1536,128]{1,0:T(8,128)} %bitcast.5, f32[1536,128]{1,0:T(8,128)} %bitcast.6, s32[512,128]{1,0:T(8,128)} %bitcast.8), custom_call_target="tpu_custom_call" | custom-call | tf_op jit(solution)/shard_map/pallas_call | solution.py:472
  72.3 0.0 copy-start
  72.3 2.1 %copy.7 = f32[3,32,16,128]{3,2,1,0:T(8,128)} copy(f32[3,32,16,128]{3,2,1,0:T(8,128)} %bitcast.7) | data formatting | bytes 1572864
  74.4 0.0 copy-done
  74.4 0.7 copy.8
Async XLA Ops:
  72.3 2.1 %copy-start = (f32[512,128]{1,0:T(8,128)S(1)}, f32[512,128]{1,0:T(8,128)}, u32[]{:S(2)}) copy-start(f32[512,128]{1,0:T(8,128)} %get-tuple-element.5) | copy-start | bytes 786436
where the time goes:
time: 75.3 us; the launch traced here: 75.1 us
  Pallas kernels  71.6 us (95%)
  local copies, waits for them, and re-layouts  2.81 us (4%)
    pallas_call x1, Pallas kernels, body(): pl.pallas_call(functools.partial(kernel, nx_dev, ny_dev, nz, nx, ny), out...  71.6 us
    unnamed x4, local copies, waits for them, and re-layouts  2.81 us

commit v1 on v0

v1 whole, which is shorter than its diff:
```python
import functools

import jax
import jax.numpy as jnp
from jax import lax
from jax.experimental import pallas as pl
from jax.experimental.pallas import tpu as pltpu
from jax.sharding import PartitionSpec as P

LEVELS = 3
SWEEPS = 2
COARSE_SWEEPS = 8
VISCOSITY = 0.1
TIME_STEP = 0.25
WEIGHT_NEW = 15.0 / 16.0
WEIGHT_OLD = -25.0 / 48.0
HELMHOLTZ = 0.0001

LANES = 128
SUB = 8
HALO_X = 8
HALO_Y = 8
HALO_1 = 16
MESH = pl.DeviceIdType.MESH


def iota2(shape, dim):
    return lax.broadcasted_iota(jnp.int32, shape, dim)


def mm(a, b):
    return jnp.dot(a, b, precision=lax.Precision.HIGHEST, preferred_element_type=jnp.float32)


class Level:
    def __init__(self, level, nz):
        self.nz = nz
        self.scale = 1.0 / float(4**level)
        lane = iota2((SUB, LANES), 1)
        row = iota2((SUB, LANES), 0)
        self.lane = lane
        self.row = row
        z = lane % nz
        self.not_top = z < nz - 1
        self.not_bottom = z > 0
        parity = (z + lane // nz + row) % 2
        self.colour = [parity == 0, parity == 1]
        edge = (z == 0) | (z == nz - 1)
        diag_in = HELMHOLTZ + 6.0 * self.scale
        diag_edge = HELMHOLTZ + 5.0 * self.scale
        self.diag = jnp.where(edge, diag_edge, diag_in).astype(jnp.float32)
        self.inv = jnp.where(edge, 1.0 / diag_edge, 1.0 / diag_in).astype(jnp.float32)
        self.take = jnp.where(
            edge, self.scale / diag_edge, self.scale / diag_in
        ).astype(jnp.float32)

    def x_plus(self, tiles, t):
        n = len(tiles)
        both = tiles[t] if n == 1 else jnp.where(self.lane < self.nz, tiles[(t + 1) % n], tiles[t])
        return pltpu.roll(both, LANES - self.nz, 1)

    def x_minus(self, tiles, t):
        n = len(tiles)
        last = self.lane >= LANES - self.nz
        both = tiles[t] if n == 1 else jnp.where(last, tiles[(t - 1) % n], tiles[t])
        return pltpu.roll(both, self.nz, 1)

    def y_plus(self, tile, following):
        return pltpu.roll(jnp.where(self.row == 0, following, tile), SUB - 1, 0)

    def y_minus(self, tile, previous):
        return pltpu.roll(jnp.where(self.row == SUB - 1, previous, tile), 1, 0)

    def z_plus(self, tile):
        return jnp.where(self.not_top, pltpu.roll(tile, LANES - 1, 1), 0.0)

    def z_minus(self, tile):
        return jnp.where(self.not_bottom, pltpu.roll(tile, 1, 1), 0.0)


def tile_of(t):
    return slice(t * LANES, (t + 1) * LANES)


def row_loop(tiles, unroll, body):
    while tiles % unroll:
        unroll -= 1

    def step(i, carry):
        for k in range(unroll):
            body(pl.multiple_of((i * unroll + k) * SUB, SUB))
        return carry

    lax.fori_loop(0, tiles // unroll, step, 0)


class Packed:
    def __init__(self, level, nz, n):
        self.n = n
        self.half = half = nz // 2
        self.scale = scale = 1.0 / float(4**level)
        lane, row = iota2((SUB, LANES), 1), iota2((SUB, LANES), 0)
        zh = lane % half
        diag_in, diag_edge = HELMHOLTZ + 6.0 * scale, HELMHOLTZ + 5.0 * scale
        odd = ((lane // half) * n + row) % 2 == 1
        self.odd = [odd, ~odd]
        self.up, self.down, self.diag, self.inv, self.take = [], [], [], [], []
        for v in (0, 1):
            up = self.odd[v] & (zh < half - 1)
            down = self.odd[1 - v] & (zh > 0)
            inside = up | down
            self.up.append(up)
            self.down.append(down)
            self.diag.append(jnp.where(inside, diag_in, diag_edge).astype(jnp.float32))
            self.inv.append(jnp.where(inside, 1.0 / diag_in, 1.0 / diag_edge).astype(jnp.float32))
            self.take.append(jnp.where(inside, scale / diag_in, scale / diag_edge).astype(jnp.float32))

    def totals(self, q, other, r):
        n = self.n
        here = [q[other, k, pl.ds(r, SUB), :] for k in range(n)]
        first = pltpu.roll(here[0], LANES - self.half, 1)
        last = pltpu.roll(here[n - 1], self.half, 1)
        out = []
        for k in range(n):
            v = (k + 1 - other) % 2
            b = here[k]
            east = here[k + 1] if k < n - 1 else first
            west = here[k - 1] if k > 0 else last
            north = q[other, k, pl.ds(r + 1, SUB), :]
            south = q[other, k, pl.ds(r - 1, SUB), :]
            z = jnp.where(
                self.up[v],
                pltpu.roll(b, LANES - 1, 1),
                jnp.where(self.down[v], pltpu.roll(b, 1, 1), 0.0),
            )
            out.append((east + west) + (north + south) + (b + z))
        return out

    def first(self, q, f, start, count, unroll):
        def body(i):
            for k in range(self.n):
                r = i + start
                q[0, k, pl.ds(r + SUB, SUB), :] = f[0, k, pl.ds(r, SUB), :] * self.inv[k % 2]

        row_loop(count, unroll, body)

    def half_sweep(self, q, f, c, start, count, unroll, wrap):
        if wrap:
            wrap_rows(q, 1 - c)

        def body(i):
            r = i + start
            total = self.totals(q, 1 - c, r + SUB)
            for k in range(self.n):
                v = (k + c) % 2
                q[c, k, pl.ds(r + SUB, SUB), :] = (
                    f[c, k, pl.ds(r, SUB), :] * self.inv[v] + total[k] * self.take[v]
                )

        row_loop(count, unroll, body)

    def presmooth(self, q, f, sweeps, count, unroll, wrap):
        self.first(q, f, 0, count, unroll)
        for k in range(1, 2 * sweeps):
            self.half_sweep(q, f, k % 2, 0, count, unroll, wrap)

    def postsmooth(self, q, f, start, count, unroll, wrap):
        for k in range(2 * SWEEPS):
            self.half_sweep(q, f, k % 2, start, count, unroll, wrap)

    def residual(self, q, f, out, start, count, unroll, wrap):
        if wrap:
            wrap_rows(q, 0)
            wrap_rows(q, 1)
        n = self.n

        def body(i):
            r = i + start
            parts = [None] * n
            for c in (0, 1):
                total = self.totals(q, 1 - c, r + SUB)
                for k in range(n):
                    v = (k + c) % 2
                    res = f[c, k, pl.ds(r, SUB), :] - (
                        self.diag[v] * q[c, k, pl.ds(r + SUB, SUB), :] - self.scale * total[k]
                    )
                    parts[k] = res if c == 0 else parts[k] + res
            if n == 1:
                out[0, pl.ds(i, SUB), :] = parts[0]
            else:
                for j in range(n // 2):
                    out[j, pl.ds(i, SUB), :] = parts[2 * j] + parts[2 * j + 1]

        row_loop(count, unroll, body)

    def colours(self, even, odd, k):
        rows = even.shape[0]
        odd_cell = jnp.concatenate([self.odd[k % 2]] * (rows // SUB), axis=0)
        return jnp.where(odd_cell, odd, even), jnp.where(odd_cell, even, odd)


def wrap_rows(q, c):
    rows = q.shape[2]
    for k in range(q.shape[1]):
        q[c, k, 0:SUB, :] = q[c, k, rows - 2 * SUB : rows - SUB, :]
        q[c, k, rows - SUB : rows, :] = q[c, k, SUB : 2 * SUB, :]


def pair_rows(ref, j, rows):
    return ref[j, pl.ds(0, rows, stride=2), :] + ref[j, pl.ds(1, rows, stride=2), :]


def twice_rows(value, pairs, j):
    rows = value.shape[0]
    pairs[j, pl.ds(0, rows, stride=2), :] = value
    pairs[j, pl.ds(1, rows, stride=2), :] = value


def matrix(rows, cols, weight, hit):
    i, o = iota2((rows, cols), 0), iota2((rows, cols), 1)
    return jnp.where(hit(i, o), weight, 0.0).astype(jnp.float32)


def kernel(
    nx_dev, ny_dev, nz, nx, ny,
    vel_in, old_in, obs_in, cor_out, pre_out,
    vel, old, fluid, edge, edge_in, pred,
    f0, fn, hn, f0q, p0, cs, cr, gath, f1, p1, m2, f2, p2, f3, p3, pairs,
    predn, pn, gn, send_sem, recv_sem,
):
    gx, gy = lax.axis_index("gx"), lax.axis_index("gy")

    def device(dx, dy):
        return (lax.rem(gx + dx + nx_dev, nx_dev), lax.rem(gy + dy + ny_dev, ny_dev))

    peers = [(d, 0) for d in range(1, nx_dev)] + [(0, d) for d in range(1, ny_dev)]
    peers += [(a, b) for a in range(1, nx_dev) for b in (-1, 1)]
    barrier = pltpu.get_barrier_semaphore()
    for dx, dy in peers:
        pl.semaphore_signal(barrier, inc=1, device_id=device(dx, dy), device_id_type=MESH)

    number = [0]

    def send(src, dst, dx, dy):
        k = number[0]
        number[0] += 1
        copy = pltpu.make_async_remote_copy(
            src_ref=src, dst_ref=dst, send_sem=send_sem.at[k], recv_sem=recv_sem.at[k],
            device_id=device(dx, dy), device_id_type=MESH,
        )
        copy.start()
        return copy

    per = LANES // nz
    blocks = nx // per
    width = blocks * LANES
    lv0 = Level(0, nz)
    lane = lv0.lane

    def load_tile(ref, base, t):
        rows = [ref[pl.ds(base + t * per + i, nz, stride=nx), :] for i in range(per)]
        return jnp.concatenate(rows, axis=0).T

    for c in range(3):
        for t in range(blocks):
            vel[c, SUB : SUB + ny, tile_of(t + 1)] = load_tile(vel_in, c * nz * nx, t)

    pltpu_wait = functools.partial(pl.semaphore_wait, barrier)
    pltpu_wait(len(peers))

    def join(high):
        parts = []
        for c in range(3):
            source = vel[c, SUB : SUB + ny, tile_of(blocks if high else 1)]
            start = LANES - nz if high else 0
            parts.append(pltpu.roll(source, (c * nz - start) % LANES, 1))
        wide = iota2((ny, LANES), 1)
        return jnp.where(wide < nz, parts[0], jnp.where(wide < 2 * nz, parts[1], parts[2]))

    copies = [
        send(vel.at[:, ny : ny + SUB, LANES : LANES + width], vel.at[:, 0:SUB, LANES : LANES + width], 0, 1),
        send(
            vel.at[:, SUB : 2 * SUB, LANES : LANES + width],
            vel.at[:, SUB + ny : 2 * SUB + ny, LANES : LANES + width], 0, -1,
        ),
    ]
    edge[0] = join(True)
    copies.append(send(edge.at[0], edge_in.at[0], 1, 0))
    edge[1] = join(False)
    copies.append(send(edge.at[1], edge_in.at[1], -1, 0))

    for c in range(3):
        for t in range(blocks):
            old[c, :, tile_of(t)] = load_tile(old_in, c * nz * nx, t)
    for t in range(blocks):
        fluid[:, tile_of(t)] = (1 - load_tile(obs_in, 0, t)).astype(jnp.float32)
    for copy in copies:
        copy.wait()
    for c in range(3):
        vel[c, SUB : SUB + ny, tile_of(0)] = pltpu.roll(edge_in[0], (LANES - nz - c * nz) % LANES, 1)
        vel[c, SUB : SUB + ny, tile_of(blocks + 1)] = pltpu.roll(edge_in[1], (-c * nz) % LANES, 1)

    def momentum(r):
        here = [
            [vel[c, pl.ds(r + SUB, SUB), tile_of(t)] for t in range(blocks + 2)] for c in range(3)
        ]
        for t in range(1, blocks + 1):
            cols = tile_of(t)
            wet = fluid[pl.ds(r, SUB), tile_of(t - 1)]
            for c in range(3):
                q = here[c][t]
                xp, xm = lv0.x_plus(here[c], t), lv0.x_minus(here[c], t)
                yp = lv0.y_plus(q, vel[c, pl.ds(r + 2 * SUB, SUB), cols])
                ym = lv0.y_minus(q, vel[c, pl.ds(r, SUB), cols])
                zp, zm = lv0.z_plus(q), lv0.z_minus(q)
                advect = 0.5 * (
                    here[0][t] * (xp - xm) + here[1][t] * (yp - ym) + here[2][t] * (zp - zm)
                )
                diffuse = xp + xm + yp + ym + zp + zm - 6.0 * q
                tendency = VISCOSITY * diffuse - advect
                pred[c, pl.ds(r + SUB, SUB), cols] = wet * (
                    q
                    + TIME_STEP
                    * (WEIGHT_NEW * tendency + WEIGHT_OLD * old[c, pl.ds(r, SUB), tile_of(t - 1)])
                )

    row_loop(ny // SUB, 2, momentum)

    inner = slice(LANES, LANES + width)
    copies = [
        send(pred.at[0, SUB : SUB + ny, tile_of(blocks)], pred.at[0, SUB : SUB + ny, tile_of(0)], 1, 0),
        send(pred.at[0, SUB : SUB + ny, tile_of(1)], pred.at[0, SUB : SUB + ny, tile_of(blocks + 1)], -1, 0),
        send(pred.at[1, ny : ny + SUB, inner], pred.at[1, 0:SUB, inner], 0, 1),
        send(pred.at[1, SUB : 2 * SUB, inner], pred.at[1, SUB + ny : 2 * SUB + ny, inner], 0, -1),
    ]
    for copy in copies:
        copy.wait()

    side = HALO_X // per

    def divergence(r):
        u = [pred[0, pl.ds(r + SUB, SUB), tile_of(t)] for t in range(blocks + 2)]
        for t in range(1, blocks + 1):
            cols = tile_of(t)
            v = pred[1, pl.ds(r + SUB, SUB), cols]
            w = pred[2, pl.ds(r + SUB, SUB), cols]
            v_plus = lv0.y_plus(v, pred[1, pl.ds(r + 2 * SUB, SUB), cols])
            v_minus = lv0.y_minus(v, pred[1, pl.ds(r, SUB), cols])
            total = (
                (lv0.x_plus(u, t) - lv0.x_minus(u, t))
                + (v_plus - v_minus)
                + (lv0.z_plus(w) - lv0.z_minus(w))
            )
            f0[pl.ds(r, SUB), tile_of(t - 1)] = total * (-0.5 / TIME_STEP)

    row_loop(ny // SUB, 2, divergence)

    for t in range(blocks):
        fn[t] = f0[:, tile_of(t)].T
    copies = [
        send(fn.at[blocks - side : blocks], hn.at[0:side], 1, 0),
        send(fn.at[0:side], hn.at[side : 2 * side], -1, 0),
    ]

    n0, half0 = per, nz // 2
    lv0p = Packed(0, nz, n0)
    tall0 = ny + 2 * HALO_Y
    blank = jnp.zeros((half0, ny), jnp.float32)
    spare = LANES // half0 - blocks - 2 * side

    def pack(k, e, whole):
        pick = pl.ds(k * nz + e, half0, stride=2)
        rows = []
        for j in range(side):
            rows.append(hn[j, pick, :] if whole else blank)
        for t in range(blocks):
            rows.append(fn[t, pick, :])
        for j in range(side):
            rows.append(hn[side + j, pick, :] if whole else blank)
        rows += [blank] * spare
        return jnp.concatenate(rows, axis=0).T

    def own_pack(whole):
        for k in range(n0):
            both = lv0p.colours(pack(k, 0, whole), pack(k, 1, whole), k)
            for c in (0, 1):
                f0q[c, k, HALO_Y : HALO_Y + ny, :] = both[c]

    own_pack(False)
    edges = {1: slice(ny, ny + HALO_Y), -1: slice(HALO_Y, 2 * HALO_Y)}
    ends = {1: slice(0, HALO_Y), -1: slice(ny + HALO_Y, ny + 2 * HALO_Y)}
    group = iota2((SUB, LANES), 1) // half0
    slots = LANES // half0
    corners = [(a, b) for a in (1, -1) for b in (1, -1)]
    for i, (dx, dy) in enumerate(corners):
        for j in range(side):
            own = (blocks if dx > 0 else side) + j
            out = None
            for m in range(2 * n0):
                value = f0q[m // n0, m % n0, edges[dy], :]
                value = pltpu.roll(value, ((m - own) * half0) % LANES, 1)
                out = value if out is None else jnp.where(group == m, value, out)
            cs[i, j] = out
    for dy in (1, -1):
        copies.append(send(f0q.at[:, :, edges[dy], :], cr.at[4 + (dy < 0)], 0, dy))
    for i, (dx, dy) in enumerate(corners):
        copies.append(send(cs.at[i], cr.at[i, 0, 0:side], dx, dy))

    def turn_rows(ref, base, t, turned):
        for i in range(per):
            ref[pl.ds(base + t * per + i, nz, stride=nx), :] = turned[i * nz : (i + 1) * nz, :]

    for c in range(3):
        for t in range(blocks):
            turn_rows(predn, c * nz * nx, t, pred[c, SUB : SUB + ny, tile_of(t + 1)].T)

    p0[...] = jnp.zeros(p0.shape, jnp.float32)
    p1[...] = jnp.zeros(p1.shape, jnp.float32)
    for copy in copies:
        copy.wait()

    own_pack(True)
    for dy in (1, -1):
        for m in range(2 * n0):
            value = cr[4 + (dy < 0), m // n0, m % n0]
            for i, (dx, cy) in enumerate(corners):
                if cy == dy:
                    for j in range(side):
                        g = j if dx > 0 else side + blocks + j
                        part = pltpu.roll(cr[i, 0, j], ((g - m) * half0) % LANES, 1)
                        value = jnp.where(group == g, part, value)
            f0q[m // n0, m % n0, ends[dy], :] = value

    tiles0 = tall0 // SUB
    lv0p.presmooth(p0, f0q, SWEEPS, tiles0, tiles0, False)
    lv0p.residual(p0, f0q, pairs, HALO_Y, ny // SUB, ny // SUB, False)

    own_x, nz1, half1 = nx // 2, nz // 2, nz // 4
    n1 = nx_dev * own_x * half1 // LANES
    lv1 = Packed(1, nz1, n1)
    wide = own_x // n1 * half1
    rows1 = ny // 2

    def down0(i, o):
        x = 2 * ((i % LANES) // half0 - side) + i // LANES
        z = i % half0
        place = ((z % 2) * n1 + x % n1) * wide + (x // n1) * half1 + z // 2
        return (x >= 0) & (x < own_x) & (place == o)

    sums = jnp.concatenate([pair_rows(pairs, j, rows1) for j in range(n0 // 2)], axis=1)
    gath[0, HALO_1 : HALO_1 + rows1, :] = mm(sums, matrix(LANES * (n0 // 2), LANES, 0.125, down0))
    body1 = slice(HALO_1, HALO_1 + rows1)
    copies = [send(gath.at[0, body1], gath.at[j, body1], nx_dev - j, 0) for j in range(1, nx_dev)]
    for j in range(nx_dev):
        copies.append(send(gath.at[0, rows1 : rows1 + HALO_1], gath.at[j, 0:HALO_1], nx_dev - j, 1))
        copies.append(
            send(gath.at[0, HALO_1 : 2 * HALO_1], gath.at[j, rows1 + HALO_1 : rows1 + 2 * HALO_1], nx_dev - j, -1)
        )
    for copy in copies:
        copy.wait()

    tall1 = rows1 + 2 * HALO_1
    source = iota2((SUB, LANES), 1) // wide

    def spread(r):
        parts = [gath[j, pl.ds(r, SUB), :] for j in range(nx_dev)]
        arr = []
        for m in range(2 * n1):
            out = pltpu.roll(parts[0], (-m * wide) % LANES, 1) if m else parts[0]
            for j in range(1, nx_dev):
                moved = pltpu.roll(parts[j], ((j - m) * wide) % LANES, 1) if j != m else parts[j]
                out = jnp.where(source == j, moved, out)
            arr.append(out)
        for k in range(n1):
            both = lv1.colours(arr[k], arr[n1 + k], k)
            f1[0, k, pl.ds(r, SUB), :] = both[0]
            f1[1, k, pl.ds(r, SUB), :] = both[1]

    tiles1 = tall1 // SUB
    row_loop(tiles1, tiles1, spread)
    lv1.presmooth(p1, f1, SWEEPS, tiles1, tiles1, False)
    lv1.residual(p1, f1, pairs, HALO_1, rows1 // SUB, rows1 // SUB, False)

    x2, nz2, half2 = nx_dev * nx // 4, nz // 4, nz // 8
    lanes2 = x2 * half2
    lv2 = Packed(2, nz2, 1)
    pieces = max(1, n1 // 2)
    own2 = ny // 4

    def down1(i, o):
        x = (i % LANES) // half1 * pieces + i // LANES
        z = i % half1
        return (z % 2) * lanes2 + x * half2 + z // 2 == o

    sums = jnp.concatenate([pair_rows(pairs, j, own2) for j in range(pieces)], axis=1)
    m2[0:own2, :] = mm(sums, matrix(LANES * pieces, 2 * lanes2, 0.125, down1))
    copies = [
        send(m2.at[0:own2, :], m2.at[j * own2 : (j + 1) * own2, :], 0, ny_dev - j) for j in range(1, ny_dev)
    ]
    for copy in copies:
        copy.wait()
    rows2 = ny_dev * own2
    low_half = iota2((SUB, LANES), 1) < LANES // 2

    def spread2(r):
        if lanes2 == LANES:
            even, odd = m2[pl.ds(r, SUB), 0:LANES], m2[pl.ds(r, SUB), LANES : 2 * LANES]
        else:
            both = m2[pl.ds(r, SUB), :]
            turned = pltpu.roll(both, LANES // 2, 1)
            even, odd = jnp.where(low_half, both, turned), jnp.where(low_half, turned, both)
        both = lv2.colours(even, odd, 0)
        f2[0, 0, pl.ds(r, SUB), :] = both[0]
        f2[1, 0, pl.ds(r, SUB), :] = both[1]

    row_loop(rows2 // SUB, 32, spread2)
    lv2.presmooth(p2, f2, SWEEPS, rows2 // SUB, 32, True)
    lv2.residual(p2, f2, pairs, 0, rows2 // SUB, 32, True)

    x3, half3 = x2 // 2, half2 // 2
    lv3 = Packed(3, nz2 // 2, 1)
    rows3 = rows2 // 2

    def down2(i, o):
        lane = o % LANES
        hit = (i < lanes2) & (i // half2 // 2 == (lane // half3) % x3)
        return hit & (i % half2 == 2 * (lane % half3) + o // LANES)

    down = mm(pair_rows(pairs, 0, rows3), matrix(LANES, 2 * LANES, 0.125, down2))
    both = lv3.colours(down[:, 0:LANES], down[:, LANES : 2 * LANES], 0)
    f3[0, 0] = both[0]
    f3[1, 0] = both[1]
    lv3.presmooth(p3, f3, COARSE_SWEEPS, rows3 // SUB, 16, True)

    def up3(i, o):
        lane = i % LANES
        hit = (lane < x3 * half3) & (lane // half3 == (o // half2) % x2 // 2)
        return hit & (2 * (lane % half3) + i // LANES == o % half2)

    inner3 = slice(SUB, SUB + rows3)
    both = lv3.colours(p3[0, 0, inner3, :], p3[1, 0, inner3, :], 0)
    twice_rows(mm(jnp.concatenate(both, axis=1), matrix(2 * LANES, LANES, 1.0, up3)), pairs, 0)
    p2[1, 0, SUB : SUB + rows2, :] += pairs[0, 0:rows2, :]
    lv2.postsmooth(p2, f2, 0, rows2 // SUB, 32, True)
    wrap_rows(p2, 0)
    wrap_rows(p2, 1)

    def up2(i, o):
        lane, to = i % LANES, o % LANES
        hit = (lane < lanes2) & (lane // half2 == (to // half1) * pieces + o // LANES)
        return hit & (2 * (lane % half2) + i // LANES == to % half1)

    first2 = SUB - HALO_1 // 2
    window = slice(first2, first2 + tall1 // 2)
    both = lv2.colours(p2[0, 0, window, :], p2[1, 0, window, :], 0)
    lift = mm(jnp.concatenate(both, axis=1), matrix(2 * LANES, LANES * pieces, 1.0, up2))
    for j in range(pieces):
        twice_rows(lift[:, tile_of(j)], pairs, j)
    for k in range(n1):
        p1[1, k, SUB : SUB + tall1, :] += pairs[k * pieces // n1, 0:tall1, :]
    lv1.postsmooth(p1, f1, 0, tiles1, tiles1, False)

    reach = side * n0 // 2
    wide_x = own_x + 2 * reach
    take = wide_x // n1 * half1
    off = -reach // n1 * half1
    first1 = SUB + HALO_1 - HALO_Y // 2
    window = slice(first1, first1 + tall0 // 2)
    halves = [[], []]
    for k in range(n1):
        both = lv1.colours(p1[0, k, window, :], p1[1, k, window, :], k)
        halves[0].append(both[0])
        halves[1].append(both[1])
    slot = iota2((tall0 // 2, LANES), 1) // take
    joined = []
    for e in (0, 1):
        out = None
        for k in range(n1):
            moved = pltpu.roll(halves[e][k], (k * take - off) % LANES, 1)
            out = moved if out is None else jnp.where(slot == k, moved, out)
        joined.append(out)

    def up1(i, o):
        lane, to = i % LANES, o % LANES
        x = (lane % take) // half1 * n1 + lane // take
        hit = (lane < take * n1) & (x == to // half0 * (n0 // 2) + o // LANES)
        return hit & (2 * (lane % half1) + i // LANES == to % half0)

    lift = mm(jnp.concatenate(joined, axis=1), matrix(2 * LANES, LANES * (n0 // 2), 1.0, up1))
    for j in range(n0 // 2):
        twice_rows(lift[:, tile_of(j)], pairs, j)
    for k in range(n0):
        p0[1, k, SUB : SUB + tall0, :] += pairs[k // 2, 0:tall0, :]
    lv0p.postsmooth(p0, f0q, 0, tiles0, tiles0, False)

    low = SUB + HALO_Y
    body0 = slice(low, low + ny)
    ext = nx + 2 * HALO_X
    for k in range(n0):
        value = lv0p.colours(p0[0, k, body0, :], p0[1, k, body0, :], k)
        slope = [
            p0[1 - c, k, low + 1 : low + 1 + ny, :] - p0[1 - c, k, low - 1 : low - 1 + ny, :] for c in (0, 1)
        ]
        slope = lv0p.colours(slope[0], slope[1], k)
        for e in (0, 1):
            turned, sloped = value[e].T, slope[e].T
            for b in range(side - 1, side + blocks + 1):
                part = slice(b * half0, (b + 1) * half0)
                pn[pl.ds(e * ext + b * n0 + k, half0, stride=2 * ext), :] = turned[part, :]
                if side <= b < side + blocks:
                    gn[pl.ds(e * nx + (b - side) * n0 + k, half0, stride=2 * nx), :] = sloped[part, :]

    def correct(z):
        for h in range(nx // SUB):
            def cells(dz, dx):
                return pn[pl.ds((z + dz) * ext + HALO_X + h * SUB + dx, SUB), :]

            here = pl.ds(z * nx + h * SUB, SUB)
            pre_out[here, :] = cells(0, 0)
            wet = (1 - obs_in[here, :]).astype(jnp.float32)
            above = cells(1, 0) if z < nz - 1 else 0.0
            below = cells(-1, 0) if z > 0 else 0.0
            slope = (cells(0, 1) - cells(0, -1), gn[here, :], above - below)
            for c in range(3):
                there = pl.ds(c * nz * nx + z * nx + h * SUB, SUB)
                cor_out[there, :] = wet * (predn[there, :] - (0.5 * TIME_STEP) * slope[c])

    for z in range(nz):
        correct(z)


def body(nx_dev, ny_dev, velocity, old_tendency, obstacle):
    _, nz, nx, ny = velocity.shape
    width = nx * nz
    per = LANES // nz
    blocks = nx // per
    side = HALO_X // per
    tall0 = ny + 2 * HALO_Y
    n1 = nx_dev * (nx // 2) * (nz // 4) // LANES
    tall1 = ny // 2 + 2 * HALO_1
    rows2 = ny_dev * ny // 4
    rows3 = rows2 // 2
    wide2 = 2 * (nx_dev * nx // 4) * (nz // 8)
    tall = max(tall0, tall1, rows2)
    count = max(per // 2, n1 // 2, 1)
    copies = 4 + 4 + 2 + 2 + 4 + (nx_dev - 1) + 2 * nx_dev + (ny_dev - 1)
    f32 = jnp.float32
    out = pl.pallas_call(
        functools.partial(kernel, nx_dev, ny_dev, nz, nx, ny),
        out_shape=(
            jax.ShapeDtypeStruct((3 * nz * nx, ny), f32),
            jax.ShapeDtypeStruct((nz * nx, ny), f32),
        ),
        in_specs=[pl.BlockSpec(memory_space=pltpu.VMEM)] * 3,
        out_specs=[pl.BlockSpec(memory_space=pltpu.VMEM)] * 2,
        scratch_shapes=[
            pltpu.VMEM((3, ny + 2 * SUB, width + 2 * LANES), f32),
            pltpu.VMEM((3, ny, width), f32),
            pltpu.VMEM((ny, width), f32),
            pltpu.VMEM((2, ny, LANES), f32),
            pltpu.VMEM((2, ny, LANES), f32),
            pltpu.VMEM((3, ny + 2 * SUB, width + 2 * LANES), f32),
            pltpu.VMEM((ny, width), f32),
            pltpu.VMEM((blocks, LANES, ny), f32),
            pltpu.VMEM((2 * side, LANES, ny), f32),
            pltpu.VMEM((2, per, tall0, LANES), f32),
            pltpu.VMEM((2, per, tall0 + 2 * SUB, LANES), f32),
            pltpu.VMEM((4, side, SUB, LANES), f32),
            pltpu.VMEM((6, 2, per, SUB, LANES), f32),
            pltpu.VMEM((nx_dev, tall1, LANES), f32),
            pltpu.VMEM((2, n1, tall1, LANES), f32),
            pltpu.VMEM((2, n1, tall1 + 2 * SUB, LANES), f32),
            pltpu.VMEM((rows2, wide2), f32),
            pltpu.VMEM((2, 1, rows2, LANES), f32),
            pltpu.VMEM((2, 1, rows2 + 2 * SUB, LANES), f32),
            pltpu.VMEM((2, 1, rows3, LANES), f32),
            pltpu.VMEM((2, 1, rows3 + 2 * SUB, LANES), f32),
            pltpu.VMEM((count, tall, LANES), f32),
            pltpu.VMEM((3 * nz * nx, ny), f32),
            pltpu.VMEM((nz * (nx + 2 * HALO_X), ny), f32),
            pltpu.VMEM((nz * nx, ny), f32),
            pltpu.SemaphoreType.DMA((copies,)),
            pltpu.SemaphoreType.DMA((copies,)),
        ],
        compiler_params=pltpu.CompilerParams(
            collective_id=0, has_side_effects=True, vmem_limit_bytes=60 * 1024 * 1024
        ),
    )(
        velocity.reshape(3 * nz * nx, ny),
        old_tendency.reshape(3 * nz * nx, ny),
        obstacle.reshape(nz * nx, ny),
    )
    return out[0].reshape(3, nz, nx, ny), out[1].reshape(nz, nx, ny)


def solution(mesh):
    placed = (P(None, None, "gx", "gy"), P(None, None, "gx", "gy"), P(None, "gx", "gy"))
    return jax.shard_map(
        functools.partial(body, mesh.shape["gx"], mesh.shape["gy"]),
        mesh=mesh,
        in_specs=placed,
        out_specs=(P(None, None, "gx", "gy"), P(None, "gx", "gy")),
        check_vma=False,
    )
```

time: 75.3 us -> 52.5 us (0.70)
  Pallas kernels: 71.6 us -> 48.9 us
    pallas_call x1, Pallas kernels: 71.6 us -> 48.9 us  [body(): pl.pallas_call(functools.partial(kernel, nx_dev, ny_dev, nz, nx, ny), out...]
where the time goes in v1:
time: 52.5 us; the launch traced here: 52.4 us
  Pallas kernels  48.9 us (93%)
  local copies, waits for them, and re-layouts  2.81 us (5%)
  between operations  0.65 us (1%)
    pallas_call x1, Pallas kernels, body(): pl.pallas_call(functools.partial(kernel, nx_dev, ny_dev, nz, nx, ny), out...  48.9 us
    unnamed x4, local copies, waits for them, and re-layouts  2.81 us

profile of v1, /device:TPU:0, one launch (start us, length us, event | category | flops | bytes accessed | tf_op | source)
XLA Modules:
  0.0 52.4 jit_solution(3015222559942036820)
XLA Ops:
  0.6 48.9 %shard_map.50 = (f32[1536,128]{1,0:T(8,128)}, f32[512,128]{1,0:T(8,128)}) custom-call(f32[1536,128]{1,0:T(8,128)} %bitcast.5, f32[1536,128]{1,0:T(8,128)} %bitcast.6, s32[512,128]{1,0:T(8,128)} %bitcast.8), custom_call_target="tpu_custom_call" | custom-call | tf_op jit(solution)/shard_map/pallas_call | solution.py:648
  49.6 0.0 copy-start
  49.6 2.1 %copy.7 = f32[3,32,16,128]{3,2,1,0:T(8,128)} copy(f32[3,32,16,128]{3,2,1,0:T(8,128)} %bitcast.7) | data formatting | bytes 1572864
  51.7 0.0 copy-done
  51.7 0.7 %copy.8 = f32[32,16,128]{2,1,0:T(8,128)} copy(f32[32,16,128]{2,1,0:T(8,128)S(1)} %bitcast.9) | data formatting | bytes 524288
Async XLA Ops:
  49.6 2.1 %copy-start = (f32[512,128]{1,0:T(8,128)S(1)}, f32[512,128]{1,0:T(8,128)}, u32[]{:S(2)}) copy-start(f32[512,128]{1,0:T(8,128)} %get-tuple-element.5) | copy-start | bytes 786436

commit v2 on v1

--- a/solution.py
+++ b/solution.py
@@ -225,8 +225,8 @@
     nx_dev, ny_dev, nz, nx, ny,
     vel_in, old_in, obs_in, cor_out, pre_out,
     vel, old, fluid, edge, edge_in, pred,
-    f0, fn, hn, f0q, p0, cs, cr, gath, f1, p1, m2, f2, p2, f3, p3, pairs,
-    predn, pn, gn, send_sem, recv_sem,
+    fe, fe_in, pe, pe_in, f0, fn, fs, f0q, p0, pk, pk_in, py_in,
+    gath, f1, p1, m2, f2, p2, f3, p3, pairs, predn, pn, gn, send_sem, recv_sem,
 ):
     gx, gy = lax.axis_index("gx"), lax.axis_index("gy")
 
@@ -261,6 +261,11 @@
         rows = [ref[pl.ds(base + t * per + i, nz, stride=nx), :] for i in range(per)]
         return jnp.concatenate(rows, axis=0).T
 
+    for i in (0, 1):
+        for c in range(3):
+            edge[i, c * nz : (c + 1) * nz, :] = vel_in[
+                pl.ds(c * nz * nx + (nx - 1 if i == 0 else 0), nz, stride=nx), :
+            ]
     for c in range(3):
         for t in range(blocks):
             vel[c, SUB : SUB + ny, tile_of(t + 1)] = load_tile(vel_in, c * nz * nx, t)
@@ -268,26 +273,15 @@
     pltpu_wait = functools.partial(pl.semaphore_wait, barrier)
     pltpu_wait(len(peers))
 
-    def join(high):
-        parts = []
-        for c in range(3):
-            source = vel[c, SUB : SUB + ny, tile_of(blocks if high else 1)]
-            start = LANES - nz if high else 0
-            parts.append(pltpu.roll(source, (c * nz - start) % LANES, 1))
-        wide = iota2((ny, LANES), 1)
-        return jnp.where(wide < nz, parts[0], jnp.where(wide < 2 * nz, parts[1], parts[2]))
-
     copies = [
+        send(edge.at[0], edge_in.at[0], 1, 0),
+        send(edge.at[1], edge_in.at[1], -1, 0),
         send(vel.at[:, ny : ny + SUB, LANES : LANES + width], vel.at[:, 0:SUB, LANES : LANES + width], 0, 1),
         send(
             vel.at[:, SUB : 2 * SUB, LANES : LANES + width],
             vel.at[:, SUB + ny : 2 * SUB + ny, LANES : LANES + width], 0, -1,
         ),
     ]
-    edge[0] = join(True)
-    copies.append(send(edge.at[0], edge_in.at[0], 1, 0))
-    edge[1] = join(False)
-    copies.append(send(edge.at[1], edge_in.at[1], -1, 0))
 
     for c in range(3):
         for t in range(blocks):
@@ -296,9 +290,11 @@
         fluid[:, tile_of(t)] = (1 - load_tile(obs_in, 0, t)).astype(jnp.float32)
     for copy in copies:
         copy.wait()
+    rest = jnp.zeros((LANES - 3 * nz, ny), jnp.float32)
+    beside = [jnp.concatenate([edge_in[i], rest], axis=0).T for i in (0, 1)]
     for c in range(3):
-        vel[c, SUB : SUB + ny, tile_of(0)] = pltpu.roll(edge_in[0], (LANES - nz - c * nz) % LANES, 1)
-        vel[c, SUB : SUB + ny, tile_of(blocks + 1)] = pltpu.roll(edge_in[1], (-c * nz) % LANES, 1)
+        vel[c, SUB : SUB + ny, tile_of(0)] = pltpu.roll(beside[0], (LANES - nz - c * nz) % LANES, 1)
+        vel[c, SUB : SUB + ny, tile_of(blocks + 1)] = pltpu.roll(beside[1], (-c * nz) % LANES, 1)
 
     def momentum(r):
         here = [
@@ -327,109 +323,116 @@
     row_loop(ny // SUB, 2, momentum)
 
     inner = slice(LANES, LANES + width)
+    own_rows = slice(SUB, SUB + ny)
+    factor = 0.5 / TIME_STEP
+    side = HALO_X // per
+    none = jnp.zeros((SUB, LANES), jnp.float32)
+
+    def source_of(r, t, whole):
+        cols = tile_of(t)
+        rows = pl.ds(r, SUB)
+        first, last = r == (0 if whole else SUB), r == (SUB + ny if whole else ny)
+        u = [pred[0, rows, tile_of(i)] for i in range(blocks + 2)] if whole else (
+            [none] + [pred[0, rows, tile_of(i)] for i in range(1, blocks + 1)] + [none]
+        )
+        v, w = pred[1, rows, cols], pred[2, rows, cols]
+        north = none if last else pred[1, pl.ds(r + SUB, SUB), cols]
+        south = none if first else pred[1, pl.ds(r - SUB, SUB), cols]
+        total = (
+            (lv0.x_plus(u, t) - lv0.x_minus(u, t))
+            + (lv0.y_plus(v, north) - lv0.y_minus(v, south))
+            + (lv0.z_plus(w) - lv0.z_minus(w))
+        )
+        return total * (-factor)
+
+    def turn_rows(ref, base, t, turned):
+        for i in range(per):
+            ref[pl.ds(base + t * per + i, nz, stride=nx), :] = turned[i * nz : (i + 1) * nz, :]
+
     copies = [
-        send(pred.at[0, SUB : SUB + ny, tile_of(blocks)], pred.at[0, SUB : SUB + ny, tile_of(0)], 1, 0),
-        send(pred.at[0, SUB : SUB + ny, tile_of(1)], pred.at[0, SUB : SUB + ny, tile_of(blocks + 1)], -1, 0),
-        send(pred.at[1, ny : ny + SUB, inner], pred.at[1, 0:SUB, inner], 0, 1),
-        send(pred.at[1, SUB : 2 * SUB, inner], pred.at[1, SUB + ny : 2 * SUB + ny, inner], 0, -1),
+        send(pred.at[:, ny : ny + SUB, inner], pred.at[:, 0:SUB, inner], 0, 1),
+        send(pred.at[:, SUB : 2 * SUB, inner], pred.at[:, SUB + ny : 2 * SUB + ny, inner], 0, -1),
     ]
-    for copy in copies:
-        copy.wait()
-
-    side = HALO_X // per
-
-    def divergence(r):
-        u = [pred[0, pl.ds(r + SUB, SUB), tile_of(t)] for t in range(blocks + 2)]
-        for t in range(1, blocks + 1):
-            cols = tile_of(t)
-            v = pred[1, pl.ds(r + SUB, SUB), cols]
-            w = pred[2, pl.ds(r + SUB, SUB), cols]
-            v_plus = lv0.y_plus(v, pred[1, pl.ds(r + 2 * SUB, SUB), cols])
-            v_minus = lv0.y_minus(v, pred[1, pl.ds(r, SUB), cols])
-            total = (
-                (lv0.x_plus(u, t) - lv0.x_minus(u, t))
-                + (v_plus - v_minus)
-                + (lv0.z_plus(w) - lv0.z_minus(w))
+    for dx in (1, -1):
+        i, t = (0, blocks) if dx > 0 else (1, 1)
+        for r in range(0, ny, SUB):
+            fe[i, r : r + SUB, :] = source_of(r + SUB, t, False)
+        copies.append(send(fe.at[i], fe_in.at[i], dx, 0))
+        turned = pred[0, own_rows, tile_of(t)].T
+        pe[i] = turned[LANES - nz : LANES, :] if dx > 0 else turned[0:nz, :]
+        copies.append(send(pe.at[i], pe_in.at[i], dx, 0))
+        for dy in (1, -1):
+            rows = slice(ny, ny + SUB) if dy > 0 else slice(SUB, 2 * SUB)
+            there = slice(0, SUB) if dy > 0 else slice(SUB + ny, 2 * SUB + ny)
+            copies.append(
+                send(pred.at[:, rows, tile_of(t)], pred.at[:, there, tile_of(0 if dx > 0 else blocks + 1)], dx, dy)
             )
-            f0[pl.ds(r, SUB), tile_of(t - 1)] = total * (-0.5 / TIME_STEP)
-
-    row_loop(ny // SUB, 2, divergence)
-
-    for t in range(blocks):
-        fn[t] = f0[:, tile_of(t)].T
-    copies = [
-        send(fn.at[blocks - side : blocks], hn.at[0:side], 1, 0),
-        send(fn.at[0:side], hn.at[side : 2 * side], -1, 0),
-    ]
+            copies.append(
+                send(pred.at[1, rows, tile_of(t)], pred.at[1, rows, tile_of(0 if dx > 0 else blocks + 1)], dx, 0)
+            )
 
     n0, half0 = per, nz // 2
     lv0p = Packed(0, nz, n0)
     tall0 = ny + 2 * HALO_Y
     blank = jnp.zeros((half0, ny), jnp.float32)
-    spare = LANES // half0 - blocks - 2 * side
-
-    def pack(k, e, whole):
-        pick = pl.ds(k * nz + e, half0, stride=2)
-        rows = []
-        for j in range(side):
-            rows.append(hn[j, pick, :] if whole else blank)
-        for t in range(blocks):
-            rows.append(fn[t, pick, :])
-        for j in range(side):
-            rows.append(hn[side + j, pick, :] if whole else blank)
-        rows += [blank] * spare
-        return jnp.concatenate(rows, axis=0).T
-
-    def own_pack(whole):
-        for k in range(n0):
-            both = lv0p.colours(pack(k, 0, whole), pack(k, 1, whole), k)
-            for c in (0, 1):
-                f0q[c, k, HALO_Y : HALO_Y + ny, :] = both[c]
-
-    own_pack(False)
-    edges = {1: slice(ny, ny + HALO_Y), -1: slice(HALO_Y, 2 * HALO_Y)}
-    ends = {1: slice(0, HALO_Y), -1: slice(ny + HALO_Y, ny + 2 * HALO_Y)}
     group = iota2((SUB, LANES), 1) // half0
     slots = LANES // half0
     corners = [(a, b) for a in (1, -1) for b in (1, -1)]
-    for i, (dx, dy) in enumerate(corners):
-        for j in range(side):
-            own = (blocks if dx > 0 else side) + j
-            out = None
-            for m in range(2 * n0):
-                value = f0q[m // n0, m % n0, edges[dy], :]
-                value = pltpu.roll(value, ((m - own) * half0) % LANES, 1)
-                out = value if out is None else jnp.where(group == m, value, out)
-            cs[i, j] = out
-    for dy in (1, -1):
-        copies.append(send(f0q.at[:, :, edges[dy], :], cr.at[4 + (dy < 0)], 0, dy))
-    for i, (dx, dy) in enumerate(corners):
-        copies.append(send(cs.at[i], cr.at[i, 0, 0:side], dx, dy))
-
-    def turn_rows(ref, base, t, turned):
-        for i in range(per):
-            ref[pl.ds(base + t * per + i, nz, stride=nx), :] = turned[i * nz : (i + 1) * nz, :]
 
     for c in range(3):
         for t in range(blocks):
-            turn_rows(predn, c * nz * nx, t, pred[c, SUB : SUB + ny, tile_of(t + 1)].T)
+            turn_rows(predn, c * nz * nx, t, pred[c, own_rows, tile_of(t + 1)].T)
 
     p0[...] = jnp.zeros(p0.shape, jnp.float32)
     p1[...] = jnp.zeros(p1.shape, jnp.float32)
     for copy in copies:
         copy.wait()
 
-    own_pack(True)
-    for dy in (1, -1):
-        for m in range(2 * n0):
-            value = cr[4 + (dy < 0), m // n0, m % n0]
-            for i, (dx, cy) in enumerate(corners):
-                if cy == dy:
-                    for j in range(side):
-                        g = j if dx > 0 else side + blocks + j
-                        part = pltpu.roll(cr[i, 0, j], ((g - m) * half0) % LANES, 1)
-                        value = jnp.where(group == g, part, value)
-            f0q[m // n0, m % n0, ends[dy], :] = value
+    blanks = jnp.zeros((LANES - nz, ny), jnp.float32)
+    pred[0, own_rows, tile_of(0)] = jnp.concatenate([blanks, pe_in[0]], axis=0).T
+    pred[0, own_rows, tile_of(blocks + 1)] = jnp.concatenate([pe_in[1], blanks], axis=0).T
+    for r in range(0, tall0, SUB):
+        strip = r == 0 or r == SUB + ny
+        for t in range(blocks + 2):
+            if strip or 1 <= t <= blocks:
+                f0[r : r + SUB, tile_of(t)] = source_of(r, t, True)
+                continue
+            i = 0 if t == 0 else 1
+            value = fe_in[i, r - SUB : r, :]
+            near = pltpu.roll(
+                pred[0, r : r + SUB, tile_of(1 if i == 0 else blocks)], LANES - nz if i == 0 else nz, 1
+            )
+            if i == 0:
+                value = value - jnp.where(lane >= LANES - nz, factor * near, 0.0)
+            else:
+                value = value + jnp.where(lane < nz, factor * near, 0.0)
+            if r == SUB:
+                south = pltpu.roll(pred[1, 0:SUB, tile_of(t)], 1, 0)
+                value = value + jnp.where(lv0.row == 0, factor * south, 0.0)
+            if r == ny:
+                north = pltpu.roll(pred[1, SUB + ny : 2 * SUB + ny, tile_of(t)], SUB - 1, 0)
+                value = value - jnp.where(lv0.row == SUB - 1, factor * north, 0.0)
+            f0[r : r + SUB, tile_of(t)] = value
+
+    for t in range(blocks + 2):
+        fn[t] = f0[own_rows, tile_of(t)].T
+        strips = [f0[0:SUB, tile_of(t)], f0[SUB + ny : 2 * SUB + ny, tile_of(t)]]
+        fs[t] = jnp.concatenate(strips + [jnp.zeros((LANES - 2 * SUB, LANES), jnp.float32)], axis=0).T
+
+    def pack(ref, k, e):
+        rows = [blank] * (side - 1)
+        for t in range(blocks + 2):
+            rows.append(ref[t, pl.ds(k * nz + e, half0, stride=2), :])
+        rows += [blank] * (slots - len(rows))
+        return jnp.concatenate(rows, axis=0).T
+
+    for k in range(n0):
+        both = lv0p.colours(pack(fn, k, 0), pack(fn, k, 1), k)
+        ends = lv0p.colours(pack(fs, k, 0)[0 : 2 * SUB], pack(fs, k, 1)[0 : 2 * SUB], k)
+        for c in (0, 1):
+            f0q[c, k, HALO_Y : HALO_Y + ny, :] = both[c]
+            f0q[c, k, 0:HALO_Y, :] = ends[c][0:SUB]
+            f0q[c, k, HALO_Y + ny : tall0, :] = ends[c][SUB : 2 * SUB]
 
     tiles0 = tall0 // SUB
     lv0p.presmooth(p0, f0q, SWEEPS, tiles0, tiles0, False)
@@ -456,8 +459,29 @@
         copies.append(
             send(gath.at[0, HALO_1 : 2 * HALO_1], gath.at[j, rows1 + HALO_1 : rows1 + 2 * HALO_1], nx_dev - j, -1)
         )
+
+    own0 = SUB + HALO_Y
+    for i in (0, 1):
+        for r in range(0, ny, SUB):
+            rows = slice(own0 + r, own0 + r + SUB)
+            g, k = (side + blocks - 2, n0 - 1) if i == 0 else (side + 1, 0)
+            out = pltpu.roll(p0[1, k, rows, :], ((n0 - g) * half0) % LANES, 1)
+            g = side + blocks - 1 if i == 0 else side
+            for m in range(n0):
+                part = pltpu.roll(p0[1, m, rows, :], ((m - g) * half0) % LANES, 1)
+                out = jnp.where(group == m, part, out)
+            pk[i, r : r + SUB, :] = out
     for copy in copies:
         copy.wait()
+    later = [
+        send(p0.at[1, :, own0 + ny - SUB : own0 + ny, :], py_in.at[0], 0, 1),
+        send(p0.at[1, :, own0 : own0 + SUB, :], py_in.at[1], 0, -1),
+    ]
+    for dx in (1, -1):
+        i = 0 if dx > 0 else 1
+        later.append(send(pk.at[i], pk_in.at[i, HALO_Y : HALO_Y + ny], dx, 0))
+        later.append(send(pk.at[i, ny - SUB : ny], pk_in.at[i, 0:HALO_Y], dx, 1))
+        later.append(send(pk.at[i, 0:SUB], pk_in.at[i, HALO_Y + ny : tall0], dx, -1))
 
     tall1 = rows1 + 2 * HALO_1
     source = iota2((SUB, LANES), 1) // wide
@@ -589,8 +613,24 @@
     lift = mm(jnp.concatenate(joined, axis=1), matrix(2 * LANES, LANES * (n0 // 2), 1.0, up1))
     for j in range(n0 // 2):
         twice_rows(lift[:, tile_of(j)], pairs, j)
-    for k in range(n0):
-        p0[1, k, SUB : SUB + tall0, :] += pairs[k // 2, 0:tall0, :]
+    for copy in later:
+        copy.wait()
+    for r in range(0, tall0, SUB):
+        rows = slice(SUB + r, 2 * SUB + r)
+        for k in range(n0):
+            if r == 0 or r == HALO_Y + ny:
+                value = py_in[0 if r == 0 else 1, k]
+            else:
+                value = p0[1, k, rows, :]
+            for i in (0, 1):
+                g = side - 1 if i == 0 else side + blocks
+                part = pltpu.roll(pk_in[i, r : r + SUB, :], ((g - k) * half0) % LANES, 1)
+                value = jnp.where(group == g, part, value)
+                if k == (n0 - 1 if i == 0 else 0):
+                    g = side - 2 if i == 0 else side + blocks + 1
+                    part = pltpu.roll(pk_in[i, r : r + SUB, :], ((g - n0) * half0) % LANES, 1)
+                    value = jnp.where(group == g, part, value)
+            p0[1, k, rows, :] = value + pairs[k // 2, r : r + SUB, :]
     lv0p.postsmooth(p0, f0q, 0, tiles0, tiles0, False)
 
     low = SUB + HALO_Y
@@ -634,7 +674,6 @@
     width = nx * nz
     per = LANES // nz
     blocks = nx // per
-    side = HALO_X // per
     tall0 = ny + 2 * HALO_Y
     n1 = nx_dev * (nx // 2) * (nz // 4) // LANES
     tall1 = ny // 2 + 2 * HALO_1
@@ -643,7 +682,7 @@
     wide2 = 2 * (nx_dev * nx // 4) * (nz // 8)
     tall = max(tall0, tall1, rows2)
     count = max(per // 2, n1 // 2, 1)
-    copies = 4 + 4 + 2 + 2 + 4 + (nx_dev - 1) + 2 * nx_dev + (ny_dev - 1)
+    copies = 4 + 14 + 8 + (nx_dev - 1) + 2 * nx_dev + (ny_dev - 1)
     f32 = jnp.float32
     out = pl.pallas_call(
         functools.partial(kernel, nx_dev, ny_dev, nz, nx, ny),
@@ -657,16 +696,21 @@
             pltpu.VMEM((3, ny + 2 * SUB, width + 2 * LANES), f32),
             pltpu.VMEM((3, ny, width), f32),
             pltpu.VMEM((ny, width), f32),
+            pltpu.VMEM((2, 3 * nz, ny), f32),
+            pltpu.VMEM((2, 3 * nz, ny), f32),
+            pltpu.VMEM((3, ny + 2 * SUB, width + 2 * LANES), f32),
             pltpu.VMEM((2, ny, LANES), f32),
             pltpu.VMEM((2, ny, LANES), f32),
-            pltpu.VMEM((3, ny + 2 * SUB, width + 2 * LANES), f32),
-            pltpu.VMEM((ny, width), f32),
-            pltpu.VMEM((blocks, LANES, ny), f32),
-            pltpu.VMEM((2 * side, LANES, ny), f32),
+            pltpu.VMEM((2, nz, ny), f32),
+            pltpu.VMEM((2, nz, ny), f32),
+            pltpu.VMEM((tall0, width + 2 * LANES), f32),
+            pltpu.VMEM((blocks + 2, LANES, ny), f32),
+            pltpu.VMEM((blocks + 2, LANES, ny), f32),
             pltpu.VMEM((2, per, tall0, LANES), f32),
             pltpu.VMEM((2, per, tall0 + 2 * SUB, LANES), f32),
-            pltpu.VMEM((4, side, SUB, LANES), f32),
-            pltpu.VMEM((6, 2, per, SUB, LANES), f32),
+            pltpu.VMEM((2, ny, LANES), f32),
+            pltpu.VMEM((2, tall0, LANES), f32),
+            pltpu.VMEM((2, per, SUB, LANES), f32),
             pltpu.VMEM((nx_dev, tall1, LANES), f32),
             pltpu.VMEM((2, n1, tall1, LANES), f32),
             pltpu.VMEM((2, n1, tall1 + 2 * SUB, LANES), f32),

time: 52.5 us -> 46.1 us (0.88)
  Pallas kernels: 48.9 us -> 42.4 us
    pallas_call x1, Pallas kernels: 48.9 us -> 42.4 us  [body(): pl.pallas_call(functools.partial(kernel, nx_dev, ny_dev, nz, nx, ny), out...]
where the time goes in v2:
time: 46.1 us; the launch traced here: 45.9 us
  Pallas kernels  42.4 us (92%)
  local copies, waits for them, and re-layouts  2.81 us (6%)
  between operations  0.65 us (1%)
    pallas_call x1, Pallas kernels, body(): pl.pallas_call(functools.partial(kernel, nx_dev, ny_dev, nz, nx, ny), out...  42.4 us
    unnamed x4, local copies, waits for them, and re-layouts  2.81 us

profile of v2, /device:TPU:0, one launch (start us, length us, event | category | flops | bytes accessed | tf_op | source)
XLA Modules:
  0.0 45.9 jit_solution(4515045202767965015)
XLA Ops:
  0.6 42.4 %shard_map.50 = (f32[1536,128]{1,0:T(8,128)}, f32[512,128]{1,0:T(8,128)}) custom-call(f32[1536,128]{1,0:T(8,128)} %bitcast.5, f32[1536,128]{1,0:T(8,128)} %bitcast.6, s32[512,128]{1,0:T(8,128)} %bitcast.8), custom_call_target="tpu_custom_call" | custom-call | tf_op jit(solution)/shard_map/pallas_call | solution.py:687
  43.1 0.0 copy-start
  43.1 2.1 %copy.7 = f32[3,32,16,128]{3,2,1,0:T(8,128)} copy(f32[3,32,16,128]{3,2,1,0:T(8,128)} %bitcast.7) | data formatting | bytes 1572864
  45.2 0.0 copy-done
  45.2 0.7 %copy.8 = f32[32,16,128]{2,1,0:T(8,128)} copy(f32[32,16,128]{2,1,0:T(8,128)S(1)} %bitcast.9) | data formatting | bytes 524288
Async XLA Ops:
  43.1 2.1 %copy-start = (f32[512,128]{1,0:T(8,128)S(1)}, f32[512,128]{1,0:T(8,128)}, u32[]{:S(2)}) copy-start(f32[512,128]{1,0:T(8,128)} %get-tuple-element.5) | copy-start | bytes 786436

commit v3 on v2

--- a/solution.py
+++ b/solution.py
@@ -20,7 +20,7 @@
 SUB = 8
 HALO_X = 8
 HALO_Y = 8
-HALO_1 = 16
+HALO_1 = 8
 MESH = pl.DeviceIdType.MESH
 
 
@@ -223,10 +223,10 @@
 
 def kernel(
     nx_dev, ny_dev, nz, nx, ny,
-    vel_in, old_in, obs_in, cor_out, pre_out,
+    vel_in, old_in, obs_in, predn, pn, gn,
     vel, old, fluid, edge, edge_in, pred,
-    fe, fe_in, pe, pe_in, f0, fn, fs, f0q, p0, pk, pk_in, py_in,
-    gath, f1, p1, m2, f2, p2, f3, p3, pairs, predn, pn, gn, send_sem, recv_sem,
+    fe, fe_in, pe, pe_in, f0, fn, fs, f0q, p0, pk, pk_in, py_in, p1y_in,
+    gath, f1, p1, m2, f2, p2, f3, p3, pairs, send_sem, recv_sem,
 ):
     gx, gy = lax.axis_index("gx"), lax.axis_index("gy")
 
@@ -320,7 +320,7 @@
                     * (WEIGHT_NEW * tendency + WEIGHT_OLD * old[c, pl.ds(r, SUB), tile_of(t - 1)])
                 )
 
-    row_loop(ny // SUB, 2, momentum)
+    row_loop(ny // SUB, 16, momentum)
 
     inner = slice(LANES, LANES + width)
     own_rows = slice(SUB, SUB + ny)
@@ -521,6 +521,11 @@
     copies = [
         send(m2.at[0:own2, :], m2.at[j * own2 : (j + 1) * own2, :], 0, ny_dev - j) for j in range(1, ny_dev)
     ]
+    own1 = SUB + HALO_1
+    beyond = [
+        send(p1.at[1, :, own1 + rows1 - HALO_1 : own1 + rows1, :], p1y_in.at[0], 0, 1),
+        send(p1.at[1, :, own1 : own1 + HALO_1, :], p1y_in.at[1], 0, -1),
+    ]
     for copy in copies:
         copy.wait()
     rows2 = ny_dev * own2
@@ -580,7 +585,11 @@
     lift = mm(jnp.concatenate(both, axis=1), matrix(2 * LANES, LANES * pieces, 1.0, up2))
     for j in range(pieces):
         twice_rows(lift[:, tile_of(j)], pairs, j)
+    for copy in beyond:
+        copy.wait()
     for k in range(n1):
+        p1[1, k, SUB : SUB + HALO_1, :] = p1y_in[0, k]
+        p1[1, k, own1 + rows1 : own1 + rows1 + HALO_1, :] = p1y_in[1, k]
         p1[1, k, SUB : SUB + tall1, :] += pairs[k * pieces // n1, 0:tall1, :]
     lv1.postsmooth(p1, f1, 0, tiles1, tiles1, False)
 
@@ -650,6 +659,10 @@
                 if side <= b < side + blocks:
                     gn[pl.ds(e * nx + (b - side) * n0 + k, half0, stride=2 * nx), :] = sloped[part, :]
 
+
+def finish(nz, nx, predn, pn, gn, obs_in, cor_out, pre_out):
+    ext = nx + 2 * HALO_X
+
     def correct(z):
         for h in range(nx // SUB):
             def cells(dz, dx):
@@ -682,16 +695,17 @@
     wide2 = 2 * (nx_dev * nx // 4) * (nz // 8)
     tall = max(tall0, tall1, rows2)
     count = max(per // 2, n1 // 2, 1)
-    copies = 4 + 14 + 8 + (nx_dev - 1) + 2 * nx_dev + (ny_dev - 1)
+    copies = 4 + 14 + 8 + (nx_dev - 1) + 2 * nx_dev + (ny_dev - 1) + 2
     f32 = jnp.float32
-    out = pl.pallas_call(
+    parts = pl.pallas_call(
         functools.partial(kernel, nx_dev, ny_dev, nz, nx, ny),
         out_shape=(
             jax.ShapeDtypeStruct((3 * nz * nx, ny), f32),
+            jax.ShapeDtypeStruct((nz * (nx + 2 * HALO_X), ny), f32),
             jax.ShapeDtypeStruct((nz * nx, ny), f32),
         ),
         in_specs=[pl.BlockSpec(memory_space=pltpu.VMEM)] * 3,
-        out_specs=[pl.BlockSpec(memory_space=pltpu.VMEM)] * 2,
+        out_specs=[pl.BlockSpec(memory_space=pltpu.VMEM)] * 3,
         scratch_shapes=[
             pltpu.VMEM((3, ny + 2 * SUB, width + 2 * LANES), f32),
             pltpu.VMEM((3, ny, width), f32),
@@ -711,6 +725,7 @@
             pltpu.VMEM((2, ny, LANES), f32),
             pltpu.VMEM((2, tall0, LANES), f32),
             pltpu.VMEM((2, per, SUB, LANES), f32),
+            pltpu.VMEM((2, n1, HALO_1, LANES), f32),
             pltpu.VMEM((nx_dev, tall1, LANES), f32),
             pltpu.VMEM((2, n1, tall1, LANES), f32),
             pltpu.VMEM((2, n1, tall1 + 2 * SUB, LANES), f32),
@@ -720,20 +735,27 @@
             pltpu.VMEM((2, 1, rows3, LANES), f32),
             pltpu.VMEM((2, 1, rows3 + 2 * SUB, LANES), f32),
             pltpu.VMEM((count, tall, LANES), f32),
-            pltpu.VMEM((3 * nz * nx, ny), f32),
-            pltpu.VMEM((nz * (nx + 2 * HALO_X), ny), f32),
-            pltpu.VMEM((nz * nx, ny), f32),
             pltpu.SemaphoreType.DMA((copies,)),
             pltpu.SemaphoreType.DMA((copies,)),
         ],
         compiler_params=pltpu.CompilerParams(
-            collective_id=0, has_side_effects=True, vmem_limit_bytes=60 * 1024 * 1024
+            collective_id=0, has_side_effects=True, vmem_limit_bytes=28 * 1024 * 1024
         ),
     )(
         velocity.reshape(3 * nz * nx, ny),
         old_tendency.reshape(3 * nz * nx, ny),
         obstacle.reshape(nz * nx, ny),
     )
+    out = pl.pallas_call(
+        functools.partial(finish, nz, nx),
+        out_shape=(
+            jax.ShapeDtypeStruct((3 * nz * nx, ny), f32),
+            jax.ShapeDtypeStruct((nz * nx, ny), f32),
+        ),
+        in_specs=[pl.BlockSpec(memory_space=pltpu.VMEM)] * 4,
+        out_specs=[pl.BlockSpec(memory_space=pltpu.VMEM)] * 2,
+        compiler_params=pltpu.CompilerParams(vmem_limit_bytes=16 * 1024 * 1024),
+    )(*parts, obstacle.reshape(nz * nx, ny))
     return out[0].reshape(3, nz, nx, ny), out[1].reshape(nz, nx, ny)
 
 

time: 46.1 us -> 44.1 us (0.957)
  Pallas kernels: 42.4 us -> 40.1 us
    pallas_call x1, Pallas kernels: 42.4 us -> 39 us  [body(): pl.pallas_call(functools.partial(kernel, nx_dev, ny_dev, nz, nx, ny), out...]
    pallas_call x0 -> x1, Pallas kernels: none -> 1.06 us  [body(): pl.pallas_call(functools.partial(finish, nz, nx), out_shape=(jax.ShapeDty...]
    unnamed x4 -> x6, local copies, waits for them, and re-layouts: 2.81 us -> 3.21 us
where the time goes in v3:
time: 44.1 us; the launch traced here: 43.9 us
  Pallas kernels  40.1 us (91%)
  local copies, waits for them, and re-layouts  3.21 us (7%)
  between operations  0.65 us (1%)
    pallas_call x1, Pallas kernels, body(): pl.pallas_call(functools.partial(kernel, nx_dev, ny_dev, nz, nx, ny), out...  39 us
    unnamed x6, local copies, waits for them, and re-layouts  3.21 us
    pallas_call x1, Pallas kernels, body(): pl.pallas_call(functools.partial(finish, nz, nx), out_shape=(jax.ShapeDty...  1.06 us

profile of v3, /device:TPU:0, one launch (start us, length us, event | category | flops | bytes accessed | tf_op | source)
XLA Modules:
  0.0 43.9 jit_solution(14369916986800013942)
XLA Ops:
  0.6 0.0 copy-start
  0.6 0.9 %copy-done = s32[32,16,128]{2,1,0:T(8,128)S(1)} copy-done((s32[32,16,128]{2,1,0:T(8,128)S(1)}, s32[32,16,128]{2,1,0:T(8,128)}, u32[]{:S(2)}) %copy-start) | copy-done | bytes 262168
  1.6 0.0 copy-start.1
  1.6 1.1 %copy-done.1 = f32[3,32,16,128]{3,2,1,0:T(8,128)S(1)} copy-done((f32[3,32,16,128]{3,2,1,0:T(8,128)S(1)}, f32[3,32,16,128]{3,2,1,0:T(8,128)}, u32[]{:S(2)}) %copy-start.1) | copy-done | bytes 786456
  2.7 0.0 copy-start.2
  2.7 1.1 %copy-done.2 = f32[3,32,16,128]{3,2,1,0:T(8,128)S(1)} copy-done((f32[3,32,16,128]{3,2,1,0:T(8,128)S(1)}, f32[3,32,16,128]{3,2,1,0:T(8,128)}, u32[]{:S(2)}) %copy-start.2) | copy-done | bytes 786456
  3.8 39.0 %shard_map.50 = (f32[1536,128]{1,0:T(8,128)S(1)}, f32[1024,128]{1,0:T(8,128)S(1)}, f32[512,128]{1,0:T(8,128)S(1)}) custom-call(f32[1536,128]{1,0:T(8,128)S(1)} %bitcast.7, f32[1536,128]{1,0:T(8,128)S(1)} %bitcast.8, s32[512,128]{1,0:T(8,128)S(1)} %bitcast.5), custom_call_target="tpu_custom_call" | custom-call | tf_op jit(solution)/shard_map/pallas_call | solution.py:700
  42.9 1.1 %shard_map.51 = (f32[1536,128]{1,0:T(8,128)}, f32[512,128]{1,0:T(8,128)}) custom-call(f32[1536,128]{1,0:T(8,128)S(1)} %get-tuple-element.7.predn, f32[1024,128]{1,0:T(8,128)S(1)} %get-tuple-element.8.pn, f32[512,128]{1,0:T(8,128)S(1)} %get-tuple-element.9.gn, s32[512,128]{1,0:T(8,128)S(1)} %bitcast.6), custom_call_target="tpu_custom_call" | custom-call | tf_op jit(solution)/shard_map/pallas_call | solution.py:749
Async XLA Ops:
  0.6 1.0 %copy-start = (s32[32,16,128]{2,1,0:T(8,128)S(1)}, s32[32,16,128]{2,1,0:T(8,128)}, u32[]{:S(2)}) copy-start(s32[32,16,128]{2,1,0:T(8,128)} %param.5) | copy-start | bytes 786436
  1.6 1.1 %copy-start.1 = (f32[3,32,16,128]{3,2,1,0:T(8,128)S(1)}, f32[3,32,16,128]{3,2,1,0:T(8,128)}, u32[]{:S(2)}) copy-start(f32[3,32,16,128]{3,2,1,0:T(8,128)} %param.3) | copy-start | bytes 2359300
  2.7 1.1 %copy-start.2 = (f32[3,32,16,128]{3,2,1,0:T(8,128)S(1)}, f32[3,32,16,128]{3,2,1,0:T(8,128)}, u32[]{:S(2)}) copy-start(f32[3,32,16,128]{3,2,1,0:T(8,128)} %param.4) | copy-start | bytes 2359300

commit v4 on v3

--- a/solution.py
+++ b/solution.py
@@ -223,10 +223,11 @@
 
 def kernel(
     nx_dev, ny_dev, nz, nx, ny,
-    vel_in, old_in, obs_in, predn, pn, gn,
+    vel_hbm, old_hbm, obs_hbm, predn, pn, gn, wet,
+    vel_in, old_in, obs_in,
     vel, old, fluid, edge, edge_in, pred,
     fe, fe_in, pe, pe_in, f0, fn, fs, f0q, p0, pk, pk_in, py_in, p1y_in,
-    gath, f1, p1, m2, f2, p2, f3, p3, pairs, send_sem, recv_sem,
+    gath, f1, p1, m2, f2, p2, f3, p3, pairs, load_sem, send_sem, recv_sem,
 ):
     gx, gy = lax.axis_index("gx"), lax.axis_index("gy")
 
@@ -238,6 +239,13 @@
     barrier = pltpu.get_barrier_semaphore()
     for dx, dy in peers:
         pl.semaphore_signal(barrier, inc=1, device_id=device(dx, dy), device_id_type=MESH)
+
+    loads = [
+        pltpu.make_async_copy(src, dst, load_sem.at[i])
+        for i, (src, dst) in enumerate(((vel_hbm, vel_in), (old_hbm, old_in), (obs_hbm, obs_in)))
+    ]
+    for load in loads:
+        load.start()
 
     number = [0]
 
@@ -261,6 +269,7 @@
         rows = [ref[pl.ds(base + t * per + i, nz, stride=nx), :] for i in range(per)]
         return jnp.concatenate(rows, axis=0).T
 
+    loads[0].wait()
     for i in (0, 1):
         for c in range(3):
             edge[i, c * nz : (c + 1) * nz, :] = vel_in[
@@ -283,6 +292,8 @@
         ),
     ]
 
+    loads[1].wait()
+    loads[2].wait()
     for c in range(3):
         for t in range(blocks):
             old[c, :, tile_of(t)] = load_tile(old_in, c * nz * nx, t)
@@ -354,22 +365,21 @@
         send(pred.at[:, SUB : 2 * SUB, inner], pred.at[:, SUB + ny : 2 * SUB + ny, inner], 0, -1),
     ]
     for dx in (1, -1):
+        t = blocks if dx > 0 else 1
+        far = tile_of(0 if dx > 0 else blocks + 1)
+        for dy in (1, -1):
+            rows = slice(ny, ny + SUB) if dy > 0 else slice(SUB, 2 * SUB)
+            there = slice(0, SUB) if dy > 0 else slice(SUB + ny, 2 * SUB + ny)
+            copies.append(send(pred.at[:, rows, tile_of(t)], pred.at[:, there, far], dx, dy))
+            copies.append(send(pred.at[1, rows, tile_of(t)], pred.at[1, rows, far], dx, 0))
+    for dx in (1, -1):
         i, t = (0, blocks) if dx > 0 else (1, 1)
+        turned = pred[0, own_rows, tile_of(t)].T
+        pe[i] = turned[LANES - nz : LANES, :] if dx > 0 else turned[0:nz, :]
         for r in range(0, ny, SUB):
             fe[i, r : r + SUB, :] = source_of(r + SUB, t, False)
         copies.append(send(fe.at[i], fe_in.at[i], dx, 0))
-        turned = pred[0, own_rows, tile_of(t)].T
-        pe[i] = turned[LANES - nz : LANES, :] if dx > 0 else turned[0:nz, :]
         copies.append(send(pe.at[i], pe_in.at[i], dx, 0))
-        for dy in (1, -1):
-            rows = slice(ny, ny + SUB) if dy > 0 else slice(SUB, 2 * SUB)
-            there = slice(0, SUB) if dy > 0 else slice(SUB + ny, 2 * SUB + ny)
-            copies.append(
-                send(pred.at[:, rows, tile_of(t)], pred.at[:, there, tile_of(0 if dx > 0 else blocks + 1)], dx, dy)
-            )
-            copies.append(
-                send(pred.at[1, rows, tile_of(t)], pred.at[1, rows, tile_of(0 if dx > 0 else blocks + 1)], dx, 0)
-            )
 
     n0, half0 = per, nz // 2
     lv0p = Packed(0, nz, n0)
@@ -383,6 +393,7 @@
         for t in range(blocks):
             turn_rows(predn, c * nz * nx, t, pred[c, own_rows, tile_of(t + 1)].T)
 
+    wet[...] = (1 - obs_in[...]).astype(jnp.float32)
     p0[...] = jnp.zeros(p0.shape, jnp.float32)
     p1[...] = jnp.zeros(p1.shape, jnp.float32)
     for copy in copies:
@@ -660,7 +671,7 @@
                     gn[pl.ds(e * nx + (b - side) * n0 + k, half0, stride=2 * nx), :] = sloped[part, :]
 
 
-def finish(nz, nx, predn, pn, gn, obs_in, cor_out, pre_out):
+def finish(nz, nx, predn, pn, gn, wet_in, cor_out, pre_out):
     ext = nx + 2 * HALO_X
 
     def correct(z):
@@ -670,7 +681,7 @@
 
             here = pl.ds(z * nx + h * SUB, SUB)
             pre_out[here, :] = cells(0, 0)
-            wet = (1 - obs_in[here, :]).astype(jnp.float32)
+            wet = wet_in[here, :]
             above = cells(1, 0) if z < nz - 1 else 0.0
             below = cells(-1, 0) if z > 0 else 0.0
             slope = (cells(0, 1) - cells(0, -1), gn[here, :], above - below)
@@ -703,10 +714,14 @@
             jax.ShapeDtypeStruct((3 * nz * nx, ny), f32),
             jax.ShapeDtypeStruct((nz * (nx + 2 * HALO_X), ny), f32),
             jax.ShapeDtypeStruct((nz * nx, ny), f32),
+            jax.ShapeDtypeStruct((nz * nx, ny), f32),
         ),
-        in_specs=[pl.BlockSpec(memory_space=pltpu.VMEM)] * 3,
-        out_specs=[pl.BlockSpec(memory_space=pltpu.VMEM)] * 3,
+        in_specs=[pl.BlockSpec(memory_space=pltpu.HBM)] * 3,
+        out_specs=[pl.BlockSpec(memory_space=pltpu.VMEM)] * 4,
         scratch_shapes=[
+            pltpu.VMEM((3 * nz * nx, ny), f32),
+            pltpu.VMEM((3 * nz * nx, ny), f32),
+            pltpu.VMEM((nz * nx, ny), jnp.int32),
             pltpu.VMEM((3, ny + 2 * SUB, width + 2 * LANES), f32),
             pltpu.VMEM((3, ny, width), f32),
             pltpu.VMEM((ny, width), f32),
@@ -735,6 +750,7 @@
             pltpu.VMEM((2, 1, rows3, LANES), f32),
             pltpu.VMEM((2, 1, rows3 + 2 * SUB, LANES), f32),
             pltpu.VMEM((count, tall, LANES), f32),
+            pltpu.SemaphoreType.DMA((3,)),
             pltpu.SemaphoreType.DMA((copies,)),
             pltpu.SemaphoreType.DMA((copies,)),
         ],
@@ -742,9 +758,9 @@
             collective_id=0, has_side_effects=True, vmem_limit_bytes=28 * 1024 * 1024
         ),
     )(
-        velocity.reshape(3 * nz * nx, ny),
-        old_tendency.reshape(3 * nz * nx, ny),
-        obstacle.reshape(nz * nx, ny),
+        pltpu.with_memory_space_constraint(velocity.reshape(3 * nz * nx, ny), pltpu.HBM),
+        pltpu.with_memory_space_constraint(old_tendency.reshape(3 * nz * nx, ny), pltpu.HBM),
+        pltpu.with_memory_space_constraint(obstacle.reshape(nz * nx, ny), pltpu.HBM),
     )
     out = pl.pallas_call(
         functools.partial(finish, nz, nx),
@@ -755,7 +771,7 @@
         in_specs=[pl.BlockSpec(memory_space=pltpu.VMEM)] * 4,
         out_specs=[pl.BlockSpec(memory_space=pltpu.VMEM)] * 2,
         compiler_params=pltpu.CompilerParams(vmem_limit_bytes=16 * 1024 * 1024),
-    )(*parts, obstacle.reshape(nz * nx, ny))
+    )(*parts)
     return out[0].reshape(3, nz, nx, ny), out[1].reshape(nz, nx, ny)
 
 

time: 44.1 us -> 39.9 us (0.905)
  local copies, waits for them, and re-layouts: 3.21 us -> 0 us
  Pallas kernels: 40.1 us -> 39.1 us
    unnamed x6 -> x0, local copies, waits for them, and re-layouts: 3.21 us -> none
    pallas_call x1, Pallas kernels: 39 us -> 38.1 us  [body(): pl.pallas_call(functools.partial(kernel, nx_dev, ny_dev, nz, nx, ny), out...]
where the time goes in v4:
time: 39.9 us; the launch traced here: 39.8 us
  Pallas kernels  39.1 us (98%)
  between operations  0.64 us (2%)
    pallas_call x1, Pallas kernels, body(): pl.pallas_call(functools.partial(kernel, nx_dev, ny_dev, nz, nx, ny), out...  38.1 us
    pallas_call x1, Pallas kernels, body(): pl.pallas_call(functools.partial(finish, nz, nx), out_shape=(jax.ShapeDty...  1.07 us

profile of v4, /device:TPU:0, one launch (start us, length us, event | category | flops | bytes accessed | tf_op | source)
XLA Modules:
  0.0 39.8 jit_solution(14371133031511213554)
XLA Ops:
  0.6 38.1 %shard_map.50 = (f32[1536,128]{1,0:T(8,128)S(1)}, f32[1024,128]{1,0:T(8,128)S(1)}, f32[512,128]{1,0:T(8,128)S(1)}, f32[512,128]{1,0:T(8,128)S(1)}) custom-call(f32[1536,128]{1,0:T(8,128)} %bitcast.5, f32[1536,128]{1,0:T(8,128)} %bitcast.6, s32[512,128]{1,0:T(8,128)} %bitcast.7), custom_call_target="tpu_custom_call" | custom-call | tf_op jit(solution)/shard_map/pallas_call | solution.py:711
  38.7 1.1 %shard_map.51 = (f32[1536,128]{1,0:T(8,128)}, f32[512,128]{1,0:T(8,128)}) custom-call(f32[1536,128]{1,0:T(8,128)S(1)} %get-tuple-element.8.predn, f32[1024,128]{1,0:T(8,128)S(1)} %get-tuple-element.9.pn, f32[512,128]{1,0:T(8,128)S(1)} %get-tuple-element.10.gn, f32[512,128]{1,0:T(8,128)S(1)} %get-tuple-element.11.wet_in), custom_call_target="tpu_custom_call" | custom-call | tf_op jit(solution)/shard_map/pallas_call | solution.py:765

commit v5 on v4

--- a/solution.py
+++ b/solution.py
@@ -393,6 +393,9 @@
         for t in range(blocks):
             turn_rows(predn, c * nz * nx, t, pred[c, own_rows, tile_of(t + 1)].T)
 
+    for r in range(2 * SUB, ny, SUB):
+        for t in range(2, blocks):
+            f0[r : r + SUB, tile_of(t)] = source_of(r, t, True)
     wet[...] = (1 - obs_in[...]).astype(jnp.float32)
     p0[...] = jnp.zeros(p0.shape, jnp.float32)
     p1[...] = jnp.zeros(p1.shape, jnp.float32)
@@ -405,6 +408,8 @@
     for r in range(0, tall0, SUB):
         strip = r == 0 or r == SUB + ny
         for t in range(blocks + 2):
+            if 2 * SUB <= r < ny and 2 <= t < blocks:
+                continue
             if strip or 1 <= t <= blocks:
                 f0[r : r + SUB, tile_of(t)] = source_of(r, t, True)
                 continue

time: 39.9 us -> 39.8 us (level)
  no operation moved by 1% of the time
where the time goes in v5:
time: 39.8 us; the launch traced here: 39.7 us
  Pallas kernels  39 us (98%)
  between operations  0.64 us (2%)
    pallas_call x1, Pallas kernels, body(): pl.pallas_call(functools.partial(kernel, nx_dev, ny_dev, nz, nx, ny), out...  37.9 us
    pallas_call x1, Pallas kernels, body(): pl.pallas_call(functools.partial(finish, nz, nx), out_shape=(jax.ShapeDty...  1.07 us

profile of v5, /device:TPU:0, one launch (start us, length us, event | category | flops | bytes accessed | tf_op | source)
XLA Modules:
  0.0 39.7 jit_solution(16678529188004468957)
XLA Ops:
  0.6 37.9 %shard_map.50 = (f32[1536,128]{1,0:T(8,128)S(1)}, f32[1024,128]{1,0:T(8,128)S(1)}, f32[512,128]{1,0:T(8,128)S(1)}, f32[512,128]{1,0:T(8,128)S(1)}) custom-call(f32[1536,128]{1,0:T(8,128)} %bitcast.5, f32[1536,128]{1,0:T(8,128)} %bitcast.6, s32[512,128]{1,0:T(8,128)} %bitcast.7), custom_call_target="tpu_custom_call" | custom-call | tf_op jit(solution)/shard_map/pallas_call | solution.py:716
  38.6 1.1 %shard_map.51 = (f32[1536,128]{1,0:T(8,128)}, f32[512,128]{1,0:T(8,128)}) custom-call(f32[1536,128]{1,0:T(8,128)S(1)} %get-tuple-element.8.predn, f32[1024,128]{1,0:T(8,128)S(1)} %get-tuple-element.9.pn, f32[512,128]{1,0:T(8,128)S(1)} %get-tuple-element.10.gn, f32[512,128]{1,0:T(8,128)S(1)} %get-tuple-element.11.wet_in), custom_call_target="tpu_custom_call" | custom-call | tf_op jit(solution)/shard_map/pallas_call | solution.py:770
